TPU v7x, 128 devices: a 2x2x16 block of a 8x8x16 slice. The times are simulated.
128 devices in a mesh: member: 4 (over y, x), dp: 16 (over z), mp: 2 (over core).
Axes of the slice: x: 2, y: 2, z: 16, core: 2. Of those that a mesh axis runs over, the one named last changes fastest.
The devices are a block of a 8x8x16 slice.
Arguments:
- activations: bfloat16 [8192, 2048], P(('member', 'dp')), parts along dimension 0, may hold values from -6 to 6
- out_grads: bfloat16 [8192, 10240], P(('member', 'dp'), 'mp'), parts along dimension 0, may hold values from -0.19921875 to 0.19921875
- slot_table: int32 [8, 16], P(('member', 'mp')), parts along dimension 0, may hold values from 0 to 15, each once within a row
- exponent_index: int32 [8, 16], P(('member', 'mp')), parts along dimension 0, may hold values from 0 to 1
- damping_index: int32 [8, 16], P(('member', 'mp')), parts along dimension 0, may hold values from 0 to 3
Outputs:
- update: bfloat16 [8192, 10240], P('member', 'mp'), parts along dimension 0
- preconditioners: bfloat16 [8, 16, 2, 1024, 1024], P(('member', 'mp'), 'dp'), parts along dimension 0
There are 4 independent parts, one for each index of `member`. A program takes and returns all parts, laid end to end along the dimension named above; each array names one. Nothing has to cross between parts.
Inputs may be any that keep to these rules, and one draw needn't show every extreme that they name: `slot_table`: each row is a permutation of 0 to 15; slot s belongs to dp index s.
All inputs are finite; a program needn't handle non-finite values.
Results may differ from a plain program's by a relative error of at most 0.006.
The roundings to bfloat16 on the way count: a program that leaves them out, or rounds other values in their place, can miss the bound.
Values may be sent and summed in bfloat16 or wider, within the bound.
A program may use at most 192 MiB of HBM per device.

v0:
```python
import jax
import jax.numpy as jnp
from jax import lax
from jax.sharding import PartitionSpec as P

D_WIN = 2048
FF_WIN = 10240
BLK = 1024


ROOT_ORDERS = (2.0, 4.0)
DAMPINGS = (0.03, 0.1, 0.3, 1.0)


def table_value(picked, values_table):
    values = jnp.asarray(values_table, jnp.float32)
    matches = jnp.arange(len(values_table), dtype=jnp.int32) == picked
    return jnp.sum(jnp.where(matches, values, 0.0))


def half_dot(first, second):
    return jnp.dot(
        first.astype(jnp.bfloat16), second.astype(jnp.bfloat16), preferred_element_type=jnp.float32
    )


def inverse_root(statistic, root_order, quartic, damping):
    dimension = statistic.shape[0]
    identity = jnp.eye(dimension, dtype=jnp.float32)
    damped = statistic + damping * (jnp.trace(statistic) / dimension + 1.0) * identity
    current = damped * (dimension / (2.0 * jnp.trace(damped)))
    factor = ((root_order + 1.0) * identity - current) / root_order
    estimate = factor
    square = half_dot(factor, factor)
    fourth = half_dot(square, square)
    raised = jnp.where(quartic, fourth, square)
    current = half_dot(raised, current)
    factor = ((root_order + 1.0) * identity - current) / root_order
    estimate = half_dot(estimate, factor)
    return estimate.astype(jnp.bfloat16)


def precondition(act_block, grad_block, root_order, quartic, damping):
    gradient = lax.dot_general(
        act_block, grad_block, (((0,), (0,)), ((), ())), preferred_element_type=jnp.float32
    ).astype(jnp.bfloat16)
    left_stat = lax.dot_general(
        gradient, gradient, (((1,), (1,)), ((), ())), preferred_element_type=jnp.float32
    )
    right_stat = lax.dot_general(
        gradient, gradient, (((0,), (0,)), ((), ())), preferred_element_type=jnp.float32
    )
    left_root = inverse_root(left_stat, root_order, quartic, damping)
    right_root = inverse_root(right_stat, root_order, quartic, damping)
    half_step = jnp.dot(left_root, gradient, preferred_element_type=jnp.float32).astype(
        jnp.bfloat16
    )
    block_update = jnp.dot(half_step, right_root, preferred_element_type=jnp.float32).astype(
        jnp.bfloat16
    )
    return (block_update, jnp.stack([left_root, right_root]))


def per_slot(pair):
    received = pair[0]
    codes = pair[1]
    code_value = codes[0, 0, 0].astype(jnp.int32)
    exp_pick = code_value // 4
    damp_pick = code_value % 4
    root_order = table_value(exp_pick, ROOT_ORDERS)
    quartic = exp_pick == 1
    damping = table_value(damp_pick, DAMPINGS)
    piece = received[:, 0, 0, :]
    half_side = piece.shape[1] // 2
    block_update, roots = precondition(
        piece[:, :half_side], piece[:, half_side:], root_order, quartic, damping
    )
    upd_list = [block_update]
    root_list = [roots]
    return (jnp.stack(upd_list), jnp.stack(root_list))


def on_device(activations, out_grads, slot_table, exponent_index, damping_index):
    tok_count = activations.shape[0]
    row_blocks = activations.shape[1] // BLK
    half_width = out_grads.shape[1]
    col_blocks = half_width // BLK
    half_blocks = row_blocks * col_blocks
    slot_count = slot_table.shape[1]
    owners = lax.axis_size("dp")
    per_owner = slot_count // owners
    table_row = slot_table[0, :half_blocks]
    matches = table_row[None, :] == jnp.arange(slot_count, dtype=jnp.int32)[:, None]
    filled = jnp.any(matches, axis=1)
    block_ids = jnp.sum(
        jnp.where(matches, jnp.arange(half_blocks, dtype=jnp.int32)[None, :], 0), axis=1
    )
    row_ids = block_ids // col_blocks
    col_ids = block_ids % col_blocks
    act_pieces = jnp.take(activations.reshape(tok_count, row_blocks, BLK), row_ids, axis=1)
    grad_pieces = jnp.take(out_grads.reshape(tok_count, col_blocks, BLK), col_ids, axis=1)
    payload = jnp.where(
        filled[None, :, None],
        jnp.concatenate([act_pieces, grad_pieces], axis=2),
        jnp.zeros((), jnp.bfloat16),
    )
    payload = payload.reshape(tok_count, owners, per_owner, 2 * BLK)
    slot_codes = (exponent_index[0] * 4 + damping_index[0]).astype(jnp.bfloat16)
    code_rows = jnp.broadcast_to(slot_codes[None, :], (tok_count, slot_count)).reshape(
        tok_count, owners, per_owner
    )
    owned_blocks, owned_roots = per_slot(
        (
            lax.all_to_all(payload, "dp", split_axis=1, concat_axis=0, tiled=True),
            lax.all_to_all(code_rows, "dp", split_axis=1, concat_axis=0, tiled=True),
        )
    )
    blank_grid = jnp.zeros((row_blocks * BLK, half_width), jnp.bfloat16)
    canvas = blank_grid
    pieces = lax.all_gather(owned_blocks, "dp", axis=0, tiled=True)
    first = jnp.int32(0)
    for position in range(pieces.shape[0]):
        slot_id = first + position
        row_at = row_ids[slot_id] * BLK
        col_at = col_ids[slot_id] * BLK
        before = lax.dynamic_slice(canvas, (row_at, col_at), (BLK, BLK))
        chosen = jnp.where(filled[slot_id], pieces[position], before)
        canvas = lax.dynamic_update_slice(canvas, chosen, (row_at, col_at))
    owned_wide = owned_blocks.astype(jnp.float32)
    total_sq = lax.psum(jnp.sum(owned_wide * owned_wide), ("dp", "mp"))
    rescale = lax.rsqrt(total_sq / (D_WIN * FF_WIN) + 1.0)
    update = (canvas.astype(jnp.float32) * rescale).astype(jnp.bfloat16)
    return (update, owned_roots[None])


def solution(mesh):
    placed = (
        P(("member", "dp"), None),
        P(("member", "dp"), "mp"),
        P(("member", "mp"), None),
        P(("member", "mp"), None),
        P(("member", "mp"), None),
    )
    return jax.shard_map(
        on_device,
        mesh=mesh,
        in_specs=placed,
        out_specs=(P("member", "mp"), P(("member", "mp"), "dp", None, None, None)),
        check_vma=False,
    )
```

profile of v0, /device:TPU:69, one launch (start us, length us, event | category | flops | bytes accessed | tf_op | source)
XLA Modules:
  0.0 936.6 jit_solution(14262348473166114372)
XLA Ops:
  8.5 17.6 %all-to-all-start = ((bf16[128,16,1]{0,2,1:T(2,128)(2,1)}), bf16[128,16,1]{0,2,1:T(2,128)(2,1)S(1)}, u32[]{:S(2)}, u32[]{:S(2)}) async-start(bf16[128,16,1]{0,2,1:T(2,128)(2,1)} %reshape.190), calls=%async_computation | async-start | bytes 16384 | tf_op jit(solution)/shard_map/all_to_all | solution.py:115
  36.7 3.9 select_bitcast_fusion
  40.6 4.5 fusion
  45.1 11.6 %all-to-all-start.1 = ((bf16[128,16,1,2048]{3,0,2,1:T(8,128)(2,1)}), bf16[128,16,1,2048]{3,0,2,1:T(8,128)(2,1)}, u32[]{:S(2)}, u32[]{:S(2)}) async-start(bf16[128,16,1,2048]{3,0,2,1:T(8,128)(2,1)} %fusion), calls=%async_computation.1 | async-start | bytes 16777216 | tf_op jit(solution)/shard_map/all_to_all | solution.py:114
  60.0 358.2 %all-to-all-done.1 = bf16[128,16,1,2048]{3,0,2,1:T(8,128)(2,1)} async-done(((bf16[128,16,1,2048]{3,0,2,1:T(8,128)(2,1)}), bf16[128,16,1,2048]{3,0,2,1:T(8,128)(2,1)}, u32[]{:S(2)}, u32[]{:S(2)}) %all-to-all-start.1) | async-done | bytes 8388640 | tf_op jit(solution)/shard_map/all_to_all | solution.py:114
  418.2 8.0 fusion.55
  426.2 5.0 select_reduce_fusion.3
  431.2 5.0 select_reduce_fusion.1
  444.6 3.7 fusion.73
  448.3 10.9 %fusion.4 = bf16[1024,1024]{1,0:T(8,128)(2,1)} fusion(f32[1024,1024]{1,0:T(8,128)} %get-tuple-element.63, bf16[1024,1024]{1,0:T(8,128)(2,1)} %fusion.73, f32[]{:T(128)} %fusion.64, f32[]{:T(128)S(6)} %div.65, f32[]{:T(128)S(6)} %mul.257, f32[]{:T(128)S(6)} %add.216, pred[]{:T(512)S(6)} %eq.64), kind=kOutput, calls=%fused_computation.12 | convolution fusion | flops 4306501632 | bytes 8388625 | tf_op jit(solution)/shard_map/dot_general | solution.py:22
  459.2 5.2 convolution_convert_fusion.1
  472.7 3.7 fusion.74
  476.3 10.4 %fusion.8 = bf16[1024,1024]{1,0:T(8,128)(2,1)} fusion(f32[1024,1024]{1,0:T(8,128)} %get-tuple-element.61, bf16[1024,1024]{1,0:T(8,128)(2,1)} %fusion.74, f32[]{:T(128)S(6)} %div.70, f32[]{:T(128)S(6)} %mul.263, f32[]{:T(128)} %fusion.64, f32[]{:T(128)S(6)} %add.216, pred[]{:T(512)S(6)} %eq.64), kind=kOutput, calls=%fused_computation.16 | convolution fusion | flops 4306501632 | bytes 8388625 | tf_op jit(solution)/shard_map/dot_general | solution.py:22
  486.8 5.2 convolution_convert_fusion
  492.0 9.7 %multiply_reduce_fusion = (f32[]{:T(128)}, bf16[1024,1024]{1,0:T(8,128)(2,1)}) fusion(bf16[1024,1024]{1,0:T(8,128)(2,1)} %convolution_convert_fusion, bf16[1024,1024]{1,0:T(8,128)(2,1)} %convolution_convert_fusion.1, bf16[1024,1024]{1,0:T(8,128)(2,1)} %copy-done.3), kind=kOutput, calls=%fused_computation.23 | convolution fusion | flops 4300210176 | bytes 8388612 | tf_op jit(solution)/shard_map/dot_general | solution.py:58
  524.3 54.0 %psum.7 = f32[]{:T(128)} all-reduce(f32[]{:T(128)} %get-tuple-element.64), channel_id=1, replica_groups=mesh['member'=4,'dp'=16,'mp'=2] {'dp','mp'}, use_global_device_ids=true, to_apply=%region_9.10 | all-reduce | flops 1 | bytes 8 | tf_op jit(solution)/shard_map/psum | solution.py:130
  579.1 4.0 maximum_bitcast_fusion
  583.1 275.0 %all-gather.3.cloned.1.call-done = bf16[16384,1024]{1,0:T(8,128)(2,1)} async-done(((bf16[1024,1024]{1,0:T(8,128)(2,1)}), bf16[16384,1024]{1,0:T(8,128)(2,1)}) %all-gather.3.cloned.1.call-update) | async-done | bytes 33554448 | tf_op jit(solution)/shard_map/all_gather | solution.py:120
  863.9 3.7 fusion.28
  867.6 3.7 fusion.27
  871.3 3.7 fusion.26
  875.1 3.7 fusion.25
  878.7 3.7 fusion.24
  882.5 3.7 fusion.23
  886.2 3.7 fusion.22
  889.9 3.7 fusion.21
  893.6 3.9 fusion.20
  897.6 3.7 fusion.19
  901.3 3.7 fusion.18
  905.0 3.7 fusion.17
  912.3 3.7 fusion.15
  919.6 9.9 %multiply_convert_fusion = bf16[2048,5120]{1,0:T(8,128)(2,1)} fusion(bf16[2048,5120]{1,0:T(8,128)(2,1)S(1)} %fusion.14, f32[]{:T(128)S(6)} %rsqrt.3), kind=kLoop, calls=%fused_computation.2 | loop fusion | flops 31457280 | bytes 41943044 | tf_op jit(solution)/shard_map/convert_element_type | solution.py:132
  (42 shorter events, 41.8 us)
Async XLA Ops:
  8.5 36.6 %all-to-all-start = ((bf16[128,16,1]{0,2,1:T(2,128)(2,1)}), bf16[128,16,1]{0,2,1:T(2,128)(2,1)S(1)}, u32[]{:S(2)}, u32[]{:S(2)}) async-start(bf16[128,16,1]{0,2,1:T(2,128)(2,1)} %reshape.190), calls=%async_computation | async-start | bytes 16384 | tf_op jit(solution)/shard_map/all_to_all | solution.py:115
  45.1 13.1 %copy-start.2 = (f32[2]{0:T(128)S(1)}, f32[2]{0:T(128)}, u32[]{:S(2)}) copy-start(f32[2]{0:T(128)} %constant.146.clone) | copy-start | bytes 28
  45.1 14.3 %copy-start.1 = (f32[4]{0:T(128)S(1)}, f32[4]{0:T(128)}, u32[]{:S(2)}) copy-start(f32[4]{0:T(128)} %constant.147.clone) | copy-start | bytes 52
  45.1 373.1 %all-to-all-start.1 = ((bf16[128,16,1,2048]{3,0,2,1:T(8,128)(2,1)}), bf16[128,16,1,2048]{3,0,2,1:T(8,128)(2,1)}, u32[]{:S(2)}, u32[]{:S(2)}) async-start(bf16[128,16,1,2048]{3,0,2,1:T(8,128)(2,1)} %fusion), calls=%async_computation.1 | async-start | bytes 16777216 | tf_op jit(solution)/shard_map/all_to_all | solution.py:114
  56.7 801.4 %all-gather.3.cloned.1.call-start = ((), (), s32[]{:S(2)}) async-start(), calls=%async_computation.2 | async-start | bytes 35651584 | tf_op jit(solution)/shard_map/all_gather | solution.py:120
  426.2 5.0 copy-start.3
  492.0 87.0 %copy-start = (bf16[1024,1024]{1,0:T(8,128)(2,1)S(1)}, bf16[1024,1024]{1,0:T(8,128)(2,1)}, u32[]{:S(2)}) copy-start(bf16[1024,1024]{1,0:T(8,128)(2,1)} %convolution_convert_fusion.1) | copy-start | bytes 6291460
Sparse Core Ops, SparseCore 0:
  501.9 356.2 all-gather.2
where the time goes:
time: 942 us; the launch traced here: 937 us
  waiting for transfers between devices  633 us (67%)
  other arithmetic  96 us (10%)
  matrix products  66.9 us (7%)
  blocking collectives  54 us (6%)
  between operations  40.8 us (4%)
  starting transfers between devices  29.4 us (3%)
  local copies, waits for them, and re-layouts  16.2 us (2%)
    all_to_all x1, waiting for transfers between devices, on_device(): lax.all_to_all(payload, 'dp', split_axis=1, concat_axis=0, tiled=True)  358 us
    all_gather x1, waiting for transfers between devices, on_device(): pieces = lax.all_gather(owned_blocks, 'dp', axis=0, tiled=True)  275 us
    dynamic_update_slice x16, other arithmetic, on_device(): canvas = lax.dynamic_update_slice(canvas, chosen, (row_at, col_at))  58.8 us
    psum x1, blocking collectives, on_device(): total_sq = lax.psum(jnp.sum(owned_wide * owned_wide), ('dp', 'mp'))  54 us
    dot_general x6, matrix products, half_dot(): jnp.dot(first.astype(jnp.bfloat16), second.astype(jnp.bfloat16), preferre...  39.1 us
  transfers between devices with their start and end apart: 3, of which 2 were waited for; matrix products, arithmetic and copies ran while one was open for 3% of the time, Pallas kernels for 0%

commit v1 on v0

v1 whole, which is shorter than its diff:
```python
import functools

import jax
import jax.numpy as jnp
import numpy as np
from jax import lax
from jax.experimental import pallas as pl
from jax.experimental.pallas import tpu as pltpu
from jax.sharding import PartitionSpec as P

BLK = 1024
LANE = 128
ROOT_ORDERS = (2.0, 4.0)
DAMPINGS = (0.03, 0.1, 0.3, 1.0)
SHIFT = 4
MESH = pl.DeviceIdType.MESH


def table_value(picked, values_table):
    values = jnp.asarray(values_table, jnp.float32)
    matches = jnp.arange(len(values_table), dtype=jnp.int32) == picked
    return jnp.sum(jnp.where(matches, values, 0.0))


def half_dot(first, second):
    return jnp.dot(
        first.astype(jnp.bfloat16), second.astype(jnp.bfloat16), preferred_element_type=jnp.float32
    )


def inverse_root(statistic, root_order, quartic, damping):
    dimension = statistic.shape[0]
    identity = jnp.eye(dimension, dtype=jnp.float32)
    damped = statistic + damping * (jnp.trace(statistic) / dimension + 1.0) * identity
    current = damped * (dimension / (2.0 * jnp.trace(damped)))
    factor = ((root_order + 1.0) * identity - current) / root_order
    estimate = factor
    square = half_dot(factor, factor)
    fourth = half_dot(square, square)
    raised = jnp.where(quartic, fourth, square)
    current = half_dot(raised, current)
    factor = ((root_order + 1.0) * identity - current) / root_order
    estimate = half_dot(estimate, factor)
    return estimate.astype(jnp.bfloat16)


def two_roots(gradient, exp_pick, damp_pick):
    root_order = table_value(exp_pick, ROOT_ORDERS)
    quartic = exp_pick == 1
    damping = table_value(damp_pick, DAMPINGS)
    left_stat = lax.dot_general(
        gradient, gradient, (((1,), (1,)), ((), ())), preferred_element_type=jnp.float32
    )
    right_stat = lax.dot_general(
        gradient, gradient, (((0,), (0,)), ((), ())), preferred_element_type=jnp.float32
    )
    return (
        inverse_root(left_stat, root_order, quartic, damping),
        inverse_root(right_stat, root_order, quartic, damping),
    )


def greet_group(n, z, h):
    barrier = pltpu.get_barrier_semaphore()
    pl.semaphore_signal(barrier, inc=1, device_id={"mp": 1 - h}, device_id_type=MESH)
    for o in range(1, n):
        for t in range(2):
            pl.semaphore_signal(
                barrier, inc=1, device_id={"dp": lax.rem(z + o, n), "mp": t}, device_id_type=MESH
            )
    pl.semaphore_wait(barrier, 2 * n - 1)


def remote(src, dst, send, recv, **to):
    return pltpu.make_async_remote_copy(
        src_ref=src, dst_ref=dst, send_sem=send, recv_sem=recv, device_id=to, device_id_type=MESH
    )


def collect_kernel(
    n, a_in, b_in, tbl_in, a_all, b_all, tbl_out,
    as_r, ar_r, as_l, ar_l, b_send, b_recv, f_send, f_recv, t_send, t_recv, loc_sem,
):
    z = lax.axis_index("dp")
    h = lax.axis_index("mp")
    tok = a_in.shape[0]
    half = tok // 2
    right, left = lax.rem(z + 1, n), lax.rem(z + n - 1, n)
    greet_group(n, z, h)
    steps = n // 2
    top, low = pl.ds(0, half), pl.ds(half, half)
    right_sends = []
    left_sends = []

    def ring_send(step):
        if step == 0:
            src_r = src_l = a_in
            at_r = at_l = z
        else:
            at_r = lax.rem(z + n - step, n)
            at_l = lax.rem(z + step, n)
            src_r, src_l = a_all.at[at_r], a_all.at[at_l]
        dst_r, dst_l = a_all.at[at_r], a_all.at[at_l]
        if step == steps - 1:
            src_r, dst_r = src_r.at[top], dst_r.at[top]
            src_l, dst_l = src_l.at[low], dst_l.at[low]
        one = remote(src_r, dst_r, as_r.at[step], ar_r.at[step], dp=right)
        two = remote(src_l, dst_l, as_l.at[step], ar_l.at[step], dp=left)
        one.start()
        two.start()
        right_sends.append(one)
        left_sends.append(two)

    def ring_recv(step):
        at_r = lax.rem(z + n - step - 1, n)
        at_l = lax.rem(z + step + 1, n)
        dst_r, dst_l = a_all.at[at_r], a_all.at[at_l]
        if step == steps - 1:
            dst_r, dst_l = dst_r.at[top], dst_l.at[low]
        remote(dst_r, dst_r, as_r.at[step], ar_r.at[step], dp=right).wait_recv()
        remote(dst_l, dst_l, as_l.at[step], ar_l.at[step], dp=left).wait_recv()

    table = remote(tbl_in, tbl_out, t_send, t_recv, mp=1 - h)
    table.start()
    own = pltpu.make_async_copy(a_in, a_all.at[z], loc_sem)
    own.start()
    ring_send(0)
    parity = lax.rem(z + h, 2)
    h_rows = pl.ds(pl.multiple_of(h * half, half), half)
    o_rows = pl.ds(pl.multiple_of((1 - h) * half, half), half)

    def piece(i):
        chip = lax.rem(z + parity + 2 * i, n)
        block = b_in.at[chip // 2]
        same = remote(block.at[h_rows], b_all.at[z, h], b_send.at[i, 0], b_recv.at[z], dp=chip, mp=h)
        other = remote(
            block.at[o_rows], b_all.at[z, 1 - h], b_send.at[i, 1], b_recv.at[z], dp=chip, mp=1 - h
        )
        return same, other

    self_chip = parity == 0
    self_copy = pltpu.make_async_copy(
        b_in.at[z // 2].at[h_rows], b_all.at[z, h], b_recv.at[z]
    )
    order = []
    for i in range(n // 4):
        order.extend([i, n // 2 - 1 - i])
    for i in order:
        same, other = piece(i)
        if i == 0:
            @pl.when(self_chip)
            def _():
                self_copy.start()

            @pl.when(jnp.logical_not(self_chip))
            def _():
                same.start()
        else:
            same.start()
        other.start()

    def forward(at):
        got = remote(b_all.at[at, h], b_all.at[at, h], b_send.at[0, 0], b_recv.at[at], mp=1 - h)
        got.wait_recv()
        out = remote(b_all.at[at, h], b_all.at[at, h], f_send.at[at], f_recv.at[at], mp=1 - h)
        out.start()

    forward(z)
    for step in range(steps):
        ring_recv(step)
        if step < steps - 1:
            ring_send(step + 1)
        if step == steps - 1:
            forward(lax.rem(z + steps, n))
        else:
            forward(lax.rem(z + step + 1, n))
            forward(lax.rem(z + n - step - 1, n))
    for o in range(n):
        at = lax.rem(z + o, n)
        end = remote(
            b_all.at[at, 1 - h], b_all.at[at, 1 - h], f_send.at[at], f_recv.at[at], mp=1 - h
        )
        end.wait_send()
        end.wait_recv()
    for one in right_sends + left_sends:
        one.wait_send()
    for i in range(n // 2):
        same, other = piece(i)
        if i == 0:
            @pl.when(jnp.logical_not(self_chip))
            def _():
                same.wait_send()
        else:
            same.wait_send()
        other.wait_send()
    own.wait()
    table.wait()


def collect(a_part, b_part, table, n):
    tok, width = a_part.shape
    cols = b_part.shape[2]
    dma = pltpu.SemaphoreType.DMA
    vmem = pl.BlockSpec(memory_space=pltpu.VMEM)
    return pl.pallas_call(
        functools.partial(collect_kernel, n),
        out_shape=(
            jax.ShapeDtypeStruct((n, tok, width), jnp.bfloat16),
            jax.ShapeDtypeStruct((n, 2, tok // 2, cols), jnp.bfloat16),
            jax.ShapeDtypeStruct(table.shape, jnp.int32),
        ),
        in_specs=[vmem] * 3,
        out_specs=(vmem,) * 3,
        scratch_shapes=[
            dma((n // 2,)), dma((n // 2,)), dma((n // 2,)), dma((n // 2,)),
            dma((n // 2, 2)), dma((n,)), dma((n,)), dma((n,)), dma(()), dma(()), dma(()),
        ],
        compiler_params=pltpu.CompilerParams(collective_id=1, has_side_effects=True),
        name="collect",
    )(a_part, b_part, table)


def home_of(block, blocks, n):
    return (n * block) // blocks


def to_home_kernel(n, rows, cols, g_in, out, send, recv):
    z = lax.axis_index("dp")
    h = lax.axis_index("mp")
    blocks = rows * cols
    half = BLK // 2
    greet_group(n, z, h)
    m = lax.rem(z, 2)
    j = z // 2
    source = z * 2 + h
    dst = out.at[pl.ds(pl.multiple_of(h * half, half), half), pl.ds(pl.multiple_of(j * LANE, LANE), LANE)]
    moves = []
    for block in range(blocks):
        row, col = block // cols, block % cols
        home = lax.rem(home_of(block, blocks, n) + SHIFT * m, n)
        src = g_in.at[pl.ds(row * half, half), pl.ds(col * LANE, LANE)]
        mine = jnp.logical_and(home == z, h == m)
        moves.append((
            mine,
            pltpu.make_async_copy(src, dst, recv.at[source]),
            remote(src, dst, send.at[block], recv.at[source], dp=home, mp=m),
        ))
    for mine, local, far in moves:
        @pl.when(mine)
        def _():
            local.start()

        @pl.when(jnp.logical_not(mine))
        def _():
            far.start()

    spot = lax.rem(z + n - SHIFT * h, n)
    busy = functools.reduce(
        jnp.logical_or, [spot == home_of(block, blocks, n) for block in range(blocks)]
    )

    @pl.when(busy)
    def _():
        for jj in range(n // 2):
            for t in range(2):
                sem = recv.at[(2 * jj + h) * 2 + t]
                part = out.at[pl.ds(t * half, half), pl.ds(jj * LANE, LANE)]
                pltpu.make_async_copy(part, part, sem).wait()

    @pl.when(jnp.logical_not(busy))
    def _():
        out[...] = jnp.zeros_like(out)

    for mine, local, far in moves:
        @pl.when(jnp.logical_not(mine))
        def _():
            far.wait_send()


def to_home(shard, n, rows, cols):
    dma = pltpu.SemaphoreType.DMA
    vmem = pl.BlockSpec(memory_space=pltpu.VMEM)
    return pl.pallas_call(
        functools.partial(to_home_kernel, n, rows, cols),
        out_shape=jax.ShapeDtypeStruct((BLK, BLK), jnp.bfloat16),
        in_specs=[vmem],
        out_specs=vmem,
        scratch_shapes=[dma((rows * cols,)), dma((2 * n,))],
        compiler_params=pltpu.CompilerParams(collective_id=2, has_side_effects=True),
        name="to_home",
    )(shard)


PIECES = 8
KEEP = 5
BUSY_AT = (0, 1, 3, 4, 6)
IDLE_AT = (2, 5, 7)
MOVES = {
    0: ((5, -1, 2), (6, -1, 3), (7, -1, 4)),
    1: ((5, 1, 0), (6, 1, 1), (7, 1, 2)),
    3: ((5, -1, 3), (6, -1, 4), (7, 2, 0)),
    4: ((5, 1, 1), (6, 1, 2), (7, 1, 3)),
    6: ((5, -1, 4), (6, 1, 0), (7, 1, 1)),
}


def spread_kernel(n, upd, out, send, recv, loc):
    z = lax.axis_index("dp")
    h = lax.axis_index("mp")
    greet_group(n, z, h)
    spot = lax.rem(lax.rem(z + n - SHIFT * h, n), 8)
    high = BLK // PIECES
    for at in BUSY_AT:
        @pl.when(spot == at)
        def _(at=at):
            sends = []
            for index, (part, step, slot) in enumerate(MOVES[at]):
                go = remote(
                    upd.at[pl.ds(part * high, high)], out.at[slot], send.at[index], recv.at[slot],
                    dp=lax.rem(z + n + step, n),
                )
                go.start()
                sends.append(go)
            for part in range(KEEP):
                out[part] = upd[pl.ds(part * high, high), :]
            for go in sends:
                go.wait_send()

    idle = functools.reduce(jnp.logical_or, [spot == at for at in IDLE_AT])

    @pl.when(idle)
    def _():
        for slot in range(KEEP):
            pltpu.make_async_copy(out.at[slot], out.at[slot], recv.at[slot]).wait()


def spread(upd, n):
    dma = pltpu.SemaphoreType.DMA
    vmem = pl.BlockSpec(memory_space=pltpu.VMEM)
    return pl.pallas_call(
        functools.partial(spread_kernel, n),
        out_shape=jax.ShapeDtypeStruct((KEEP, BLK // PIECES, BLK), jnp.bfloat16),
        in_specs=[vmem],
        out_specs=vmem,
        scratch_shapes=[dma((3,)), dma((KEEP,)), dma(())],
        compiler_params=pltpu.CompilerParams(collective_id=3, has_side_effects=True),
        name="spread",
    )(upd)


def piece_tables(n, rows, cols):
    blocks = rows * cols
    device = np.zeros((rows, PIECES, cols), np.int32)
    slot = np.zeros((rows, PIECES, cols), np.int32)
    for block in range(blocks):
        home = home_of(block, blocks, n)
        row, col = block // cols, block % cols
        for part in range(KEEP):
            device[row, part, col] = home
            slot[row, part, col] = part
        for part, step, at in MOVES[home % 8]:
            device[row, part, col] = (home + step) % n
            slot[row, part, col] = at
    return device, slot


def place_kernel(cols, table, *refs):
    scale_ref, out = refs[cols], refs[cols + 1]
    scale = scale_ref[0]
    for col in range(cols):
        wide = refs[col][0].astype(jnp.float32)
        out[:, col * BLK:(col + 1) * BLK] = (wide * scale).astype(jnp.bfloat16)


def place(gathered, table, scale, rows, cols):
    high = BLK // PIECES
    picks = [
        pl.BlockSpec((1, high, BLK), lambda g, tab, col=col: (tab[g * cols + col], 0, 0))
        for col in range(cols)
    ]
    return pl.pallas_call(
        functools.partial(place_kernel, cols),
        out_shape=jax.ShapeDtypeStruct((rows * BLK, cols * BLK), jnp.bfloat16),
        grid_spec=pltpu.PrefetchScalarGridSpec(
            num_scalar_prefetch=1,
            grid=(rows * PIECES,),
            in_specs=picks + [pl.BlockSpec(memory_space=pltpu.SMEM)],
            out_specs=pl.BlockSpec((high, cols * BLK), lambda g, tab: (g, 0)),
        ),
        name="place",
    )(table, *([gathered] * cols), scale)


def on_device(activations, out_grads, slot_table, exponent_index, damping_index):
    n = lax.axis_size("dp")
    z = lax.axis_index("dp")
    h = lax.axis_index("mp")
    tok = activations.shape[0]
    rows = activations.shape[1] // BLK
    cols = out_grads.shape[1] // BLK
    blocks = rows * cols
    half = BLK // 2
    pieces = BLK // LANE

    act = activations.reshape(tok, rows, 2, half)
    act = jnp.where(h == 0, act[:, :, 0], act[:, :, 1]).reshape(tok, rows * half)
    grads = out_grads.reshape(tok, cols, pieces, LANE).transpose(2, 0, 1, 3)
    grads = grads.reshape(pieces, tok, cols * LANE)
    table_row = jnp.broadcast_to(
        jnp.pad(slot_table, ((0, 0), (0, LANE - n))), (8, LANE)
    ).astype(jnp.int32)
    a_all, b_all, other_table = collect(act, grads, table_row, n)

    shard = lax.dot_general(
        a_all.reshape(n * tok, rows * half), b_all.reshape(n * tok, cols * LANE),
        (((0,), (0,)), ((), ())), preferred_element_type=jnp.float32,
    ).astype(jnp.bfloat16)

    home_grad = to_home(shard, n, rows, cols)

    shard_after, home_grad = lax.optimization_barrier((shard, home_grad))
    served = jnp.where(lax.rem(z, 2) == h, slot_table[0], other_table[0, :n])[:blocks]
    hits = served[None, :] == jnp.arange(n, dtype=jnp.int32)[:, None]
    filled = jnp.any(hits, axis=1)
    picks = jnp.sum(jnp.where(hits, jnp.arange(blocks, dtype=jnp.int32)[None, :], 0), axis=1)
    by_block = shard_after.reshape(rows, half, cols, LANE).transpose(0, 2, 1, 3)
    by_block = by_block.reshape(blocks, half, LANE)
    payload = jnp.where(filled[:, None, None], jnp.take(by_block, picks, axis=0), jnp.zeros((), jnp.bfloat16))
    arrived = lax.all_to_all(payload, "dp", split_axis=0, concat_axis=0, tiled=True)

    spot = lax.rem(z + n - SHIFT * h, n)
    homes = jnp.asarray([home_of(b, blocks, n) for b in range(blocks)], jnp.int32)
    block_here = jnp.sum(jnp.where(homes == spot, jnp.arange(blocks, dtype=jnp.int32), 0))
    slot_here = jnp.sum(jnp.where(jnp.arange(n) == block_here, slot_table[0], 0))
    at_slot = jnp.arange(n, dtype=jnp.int32) == slot_here
    exp_here = jnp.sum(jnp.where(at_slot, exponent_index[0], 0))
    damp_here = jnp.sum(jnp.where(at_slot, damping_index[0], 0))
    left_root, right_root = two_roots(home_grad, exp_here, damp_here)
    half_step = jnp.dot(left_root, home_grad, preferred_element_type=jnp.float32).astype(jnp.bfloat16)
    block_update = jnp.dot(half_step, right_root, preferred_element_type=jnp.float32).astype(jnp.bfloat16)
    dense = spread(block_update, n)
    gathered = lax.all_gather(dense, "dp", axis=0, tiled=True)

    wide = dense.astype(jnp.float32)
    total_sq = lax.psum(jnp.sum(wide * wide), ("dp", "mp"))
    entries = rows * BLK * cols * BLK * lax.axis_size("mp")
    rescale = lax.rsqrt(total_sq / entries + 1.0)

    swap = arrived.reshape(n // 2, 2, half, LANE).transpose(1, 0, 2, 3)
    swap = lax.all_to_all(swap, "mp", split_axis=0, concat_axis=0, tiled=True)
    slot_grad = swap.transpose(0, 2, 1, 3).reshape(BLK, BLK)
    at_own = jnp.arange(n, dtype=jnp.int32) == z
    exp_own = jnp.sum(jnp.where(at_own, exponent_index[0], 0))
    damp_own = jnp.sum(jnp.where(at_own, damping_index[0], 0))
    roots = jnp.stack(two_roots(slot_grad, exp_own, damp_own))

    device_tab, slot_tab = piece_tables(n, rows, cols)
    table = lax.rem(jnp.asarray(device_tab) + SHIFT * h, n) * KEEP + jnp.asarray(slot_tab)
    update = place(gathered, table.reshape(-1), rescale.reshape(1), rows, cols)
    return (update, roots[None, None])


def solution(mesh):
    placed = (
        P(("member", "dp"), None),
        P(("member", "dp"), "mp"),
        P(("member", "mp"), None),
        P(("member", "mp"), None),
        P(("member", "mp"), None),
    )
    return jax.shard_map(
        on_device,
        mesh=mesh,
        in_specs=placed,
        out_specs=(P("member", "mp"), P(("member", "mp"), "dp", None, None, None)),
        check_vma=False,
    )
```

time: 942 us -> 700 us (0.74)
  waiting for transfers between devices: 633 us -> 63 us
  Pallas kernels: 0 us -> 248 us
  blocking collectives: 54 us -> 166 us
  matrix products: 66.9 us -> 135 us
  other arithmetic: 96 us -> 30.9 us
  starting transfers between devices: 29.4 us -> 6.76 us
  between operations: 40.8 us -> 25.2 us
    all_to_all x2 -> x1, waiting for transfers between devices: 358 us -> 0.01 us  [on_device(): lax.all_to_all(payload, 'dp', split_axis=0, concat_axis=0, tiled=True)]
    pallas_call x0 -> x4, Pallas kernels: none -> 248 us  [the longest x1 135 us: collect(): pl.pallas_call(functools.partial(collect_kernel, n), out_shape=(jax.Shape...]
    all_gather x1, waiting for transfers between devices: 275 us -> 63 us  [on_device(): gathered = lax.all_gather(dense, 'dp', axis=0, tiled=True)]
    psum x1, blocking collectives: 54 us -> 158 us  [on_device(): total_sq = lax.psum(jnp.sum(wide * wide), ('dp', 'mp'))]
    dynamic_update_slice x16 -> x0, other arithmetic: 58.8 us -> none  [on_device(): canvas = lax.dynamic_update_slice(canvas, chosen, (row_at, col_at))]
    dot_general x6 -> x10, matrix products: 39.1 us -> 74.9 us  [half_dot(): jnp.dot(first.astype(jnp.bfloat16), second.astype(jnp.bfloat16), preferre...]
    dot_general x4 -> x7, matrix products: 27.8 us -> 59.9 us  [the longest x1 20.7 us: on_device(): jnp.dot(left_root, home_grad, preferred_element_type=jnp.float32)]
    all_to_all x2 -> x1, starting transfers between devices: 29.2 us -> 6.7 us  [on_device(): lax.all_to_all(payload, 'dp', split_axis=0, concat_axis=0, tiled=True)]
  transfers between devices with their start and end apart: 3 -> 2, of which waited for: 2 -> 1; matrix products, arithmetic and copies ran while one was open for 3% -> 11% of each run, Pallas kernels for 0% -> 0%
where the time goes in v1:
time: 700 us; the launch traced here: 691 us
  Pallas kernels  248 us (35%)
  blocking collectives  166 us (24%)
  matrix products  135 us (19%)
  waiting for transfers between devices  63 us (9%)
  other arithmetic  30.9 us (4%)
  between operations  25.2 us (4%)
  local copies, waits for them, and re-layouts  15.8 us (2%)
    psum x1, blocking collectives, on_device(): total_sq = lax.psum(jnp.sum(wide * wide), ('dp', 'mp'))  158 us
    pallas_call x1, Pallas kernels, collect(): pl.pallas_call(functools.partial(collect_kernel, n), out_shape=(jax.Shape...  135 us
    dot_general x10, matrix products, half_dot(): jnp.dot(first.astype(jnp.bfloat16), second.astype(jnp.bfloat16), preferre...  74.9 us
    pallas_call x1, Pallas kernels, to_home(): pl.pallas_call(functools.partial(to_home_kernel, n, rows, cols), out_shap...  66.6 us
    all_gather x1, waiting for transfers between devices, on_device(): gathered = lax.all_gather(dense, 'dp', axis=0, tiled=True)  63 us
    pallas_call x1, Pallas kernels, spread(): pl.pallas_call(functools.partial(spread_kernel, n), out_shape=jax.ShapeDt...  26 us
    pallas_call x1, Pallas kernels, place(): pl.pallas_call(functools.partial(place_kernel, cols), out_shape=jax.Shape...  21 us
    dot_general x1, matrix products, on_device(): jnp.dot(left_root, home_grad, preferred_element_type=jnp.float32)  20.7 us
  transfers between devices with their start and end apart: 2, of which 1 were waited for; matrix products, arithmetic and copies ran while one was open for 11% of the time, Pallas kernels for 0%

profile of v1, /device:TPU:69, one launch (start us, length us, event | category | flops | bytes accessed | tf_op | source)
XLA Modules:
  0.0 691.3 jit_solution(199321536264714896)
XLA Ops:
  14.5 134.8 %collect.1 = (bf16[16,128,1024]{2,1,0:T(8,128)(2,1)}, bf16[16,2,64,640]{3,2,1,0:T(8,128)(2,1)}, s32[8,128]{1,0:T(8,128)}) custom-call(bf16[128,1024]{1,0:T(8,128)(2,1)} %bitcast.90, bf16[8,128,640]{2,1,0:T(8,128)(2,1)} %copy.43.b_in, s32[8,128]{1,0:T(8,128)} %broadcast_in_dim.85.tbl_in), custom_call_target="tpu_custom_call" | custom-call | tf_op jit(solution)/shard_map/collect/pallas_call | solution.py:205
  149.3 7.6 %convolution_convert_fusion.g_in = bf16[1024,640]{1,0:T(8,128)(2,1)} fusion(bf16[2048,1024]{1,0:T(8,128)(2,1)} %bitcast.93, bf16[2048,640]{1,0:T(8,128)(2,1)} %bitcast.94), kind=kOutput, calls=%fused_computation.92 | convolution fusion | flops 2685009920 | bytes 8126464 | tf_op jit(solution)/shard_map/dot_general | solution.py:414
  156.9 66.6 %to_home.1 = bf16[1024,1024]{1,0:T(8,128)(2,1)} custom-call(bf16[1024,640]{1,0:T(8,128)(2,1)} %convolution_convert_fusion.g_in), custom_call_target="tpu_custom_call" | custom-call | tf_op jit(solution)/shard_map/to_home/pallas_call | solution.py:283
  223.5 7.3 %select_reduce_fusion.7 = (f32[]{:T(128)}, f32[1024,1024]{1,0:T(8,128)}) fusion(bf16[1024,1024]{1,0:T(8,128)(2,1)} %to_home.1), kind=kOutput, calls=%fused_computation.41 | convolution fusion | flops 2150629376 | bytes 6291460 | tf_op jit(solution)/shard_map/dot_general | solution.py:51
  230.9 5.0 select_reduce_fusion.5
  246.3 2.9 select_reduce_fusion.6
  249.8 7.8 %fusion.105 = bf16[1024,1024]{1,0:T(8,128)(2,1)} fusion(f32[1024,1024]{1,0:T(8,128)} %get-tuple-element.25, f32[]{:T(128)} %get-tuple-element.13, f32[]{:T(128)S(6)} %div.64, f32[]{:T(128)S(6)} %mul.114, f32[]{:T(128)S(6)} %add.74), kind=kOutput, calls=%fused_computation.138 | convolution fusion | flops 2155872256 | bytes 6291472 | tf_op jit(solution)/shard_map/dot_general | solution.py:26
  257.7 10.5 %fusion.3 = bf16[1024,1024]{1,0:T(8,128)(2,1)} fusion(f32[1024,1024]{1,0:T(8,128)} %get-tuple-element.25, bf16[1024,1024]{1,0:T(8,128)(2,1)} %fusion.105, f32[]{:T(128)} %get-tuple-element.13, f32[]{:T(128)S(6)} %div.64, f32[]{:T(128)S(6)} %mul.114, f32[]{:T(128)S(6)} %add.74, pred[]{:T(512)S(6)} %eq.126), kind=kOutput, calls=%fused_computation.12 | convolution fusion | flops 4306501632 | bytes 8388625 | tf_op jit(solution)/shard_map/dot_general | solution.py:26
  268.2 20.7 %fusion.51 = bf16[1024,1024]{1,0:T(8,128)(2,1)} fusion(bf16[1024,1024]{1,0:T(8,128)(2,1)S(1)} %copy-done.3, bf16[1024,1024]{1,0:T(8,128)(2,1)} %fusion.3, f32[1024,1024]{1,0:T(8,128)} %get-tuple-element.25, f32[]{:T(128)} %get-tuple-element.13, f32[]{:T(128)S(6)} %div.64, f32[]{:T(128)S(6)} %mul.114, f32[]{:T(128)S(6)} %add.74), kind=kOutput, calls=%fused_computation.75 | convolution fusion | flops 4304404480 | bytes 10485776 | tf_op jit(solution)/shard_map/dot_general | solution.py:439
  290.1 2.9 select_reduce_fusion.4
  293.7 7.8 %fusion.101 = bf16[1024,1024]{1,0:T(8,128)(2,1)} fusion(f32[1024,1024]{1,0:T(8,128)} %get-tuple-element.27, f32[]{:T(128)S(6)} %div.69, f32[]{:T(128)S(6)} %mul.120, f32[]{:T(128)} %get-tuple-element.13, f32[]{:T(128)S(6)} %add.74), kind=kOutput, calls=%fused_computation.137 | convolution fusion | flops 2155872256 | bytes 6291472 | tf_op jit(solution)/shard_map/dot_general | solution.py:26
  301.6 10.6 %fusion.7 = bf16[1024,1024]{1,0:T(8,128)(2,1)} fusion(f32[1024,1024]{1,0:T(8,128)} %get-tuple-element.27, bf16[1024,1024]{1,0:T(8,128)(2,1)} %fusion.101, f32[]{:T(128)S(6)} %div.69, f32[]{:T(128)S(6)} %mul.120, f32[]{:T(128)} %get-tuple-element.13, f32[]{:T(128)S(6)} %add.74, pred[]{:T(512)S(6)} %eq.126), kind=kOutput, calls=%fused_computation.16 | convolution fusion | flops 4306501632 | bytes 8388625 | tf_op jit(solution)/shard_map/dot_general | solution.py:26
  312.2 9.3 %fusion.69.upd = bf16[1024,1024]{1,0:T(8,128)(2,1)} fusion(bf16[1024,1024]{1,0:T(8,128)(2,1)S(1)} %copy-done.13, bf16[1024,1024]{1,0:T(8,128)(2,1)} %fusion.7, f32[1024,1024]{1,0:T(8,128)} %get-tuple-element.27, f32[]{:T(128)S(6)} %div.69, f32[]{:T(128)S(6)} %mul.120, f32[]{:T(128)} %get-tuple-element.13, f32[]{:T(128)S(6)} %add.74), kind=kOutput, calls=%fused_computation.89 | convolution fusion | flops 4305453056 | bytes 10485776 | tf_op jit(solution)/shard_map/dot_general | solution.py:440
  321.5 26.0 %spread.1 = bf16[5,128,1024]{2,1,0:T(8,128)(2,1)} custom-call(bf16[1024,1024]{1,0:T(8,128)(2,1)} %fusion.69.upd), custom_call_target="tpu_custom_call" | custom-call | tf_op jit(solution)/shard_map/spread/pallas_call | solution.py:340
  350.1 3.5 copy.45
  356.4 6.7 all-to-all-start
  364.4 158.0 %psum.7 = f32[]{:T(128)} all-reduce(f32[]{:T(128)} %multiply_reduce_fusion), channel_id=1, replica_groups=mesh['member'=4,'dp'=16,'mp'=2] {'dp','mp'}, use_global_device_ids=true, to_apply=%region_11.12 | all-reduce | flops 1 | bytes 8 | tf_op jit(solution)/shard_map/psum | solution.py:445
  526.5 8.4 %all_to_all.10 = bf16[2,8,512,128]{3,1,2,0:T(8,128)(2,1)S(1)} all-to-all(bf16[2,8,512,128]{3,1,2,0:T(8,128)(2,1)S(1)} %bitcast.83), channel_id=1, replica_groups=mesh['member'=4,'dp'=16,'mp'=2] {'mp'}, dimensions={0} | all-to-all | bytes 4194304 | tf_op jit(solution)/shard_map/all_to_all | solution.py:450
  534.9 5.0 select_reduce_fusion.1
  541.1 3.0 select_reduce_fusion
  544.8 5.0 select_reduce_fusion.3
  551.0 3.0 select_reduce_fusion.2
  554.7 3.5 fusion.13
  558.2 3.7 fusion.109
  561.8 10.6 %fusion.15 = bf16[1024,1024]{1,0:T(8,128)(2,1)} fusion(f32[1024,1024]{1,0:T(8,128)} %get-tuple-element.29, bf16[1024,1024]{1,0:T(8,128)(2,1)} %fusion.109, f32[]{:T(128)S(6)} %div.79, f32[]{:T(128)S(6)} %mul.135, f32[]{:T(128)} %get-tuple-element.12, f32[]{:T(128)S(6)} %add.80, pred[]{:T(512)S(6)} %eq.137), kind=kOutput, calls=%fused_computation.24 | convolution fusion | flops 4306501632 | bytes 8388625 | tf_op jit(solution)/shard_map/dot_general | solution.py:26
  572.5 5.4 convert_bitcast_fusion
  579.6 3.7 fusion.108
  583.3 10.6 %fusion.11 = bf16[1024,1024]{1,0:T(8,128)(2,1)} fusion(f32[1024,1024]{1,0:T(8,128)} %get-tuple-element.31, bf16[1024,1024]{1,0:T(8,128)(2,1)} %fusion.108, f32[]{:T(128)} %get-tuple-element.12, f32[]{:T(128)S(6)} %div.74, f32[]{:T(128)S(6)} %mul.129, f32[]{:T(128)S(6)} %add.80, pred[]{:T(512)S(6)} %eq.137), kind=kOutput, calls=%fused_computation.20 | convolution fusion | flops 4306501632 | bytes 8388625 | tf_op jit(solution)/shard_map/dot_general | solution.py:26
  593.9 4.1 convert_bitcast_fusion.1
  598.0 2.4 maximum_bitcast_fusion
  600.4 63.0 %all-gather.2.cloned.1.call-done.refs_0_.refs_1_.refs_2_.refs_3_.refs_4_ = bf16[80,128,1024]{2,1,0:T(8,128)(2,1)} async-done(((bf16[5,128,1024]{2,1,0:T(8,128)(2,1)}), bf16[80,128,1024]{2,1,0:T(8,128)(2,1)}) %all-gather.2.cloned.1.call-update) | async-done | bytes 20971536 | tf_op jit(solution)/shard_map/all_gather | solution.py:442
  663.3 21.0 %place.1 = bf16[2048,5120]{1,0:T(8,128)(2,1)} custom-call(s32[80]{0:T(128)} %reshape.62.table, bf16[80,128,1024]{2,1,0:T(8,128)(2,1)} %all-gather.2.cloned.1.call-done.refs_0_.refs_1_.refs_2_.refs_3_.refs_4_, bf16[80,128,1024]{2,1,0:T(8,128)(2,1)} %all-gather.2.cloned.1.call-done.refs_0_.refs_1_.refs_2_.refs_3_.refs_4_, ...), custom_call_target="tpu_custom_call" | custom-call | tf_op jit(solution)/shard_map/place/pallas_call | solution.py:381
  (59 shorter events, 25.6 us)
Async XLA Ops:
  7.2 656.2 %all-gather.2.cloned.1.call-start = ((), (), s32[]{:S(2)}) async-start(), calls=%async_computation.2 | async-start | bytes 22282240 | tf_op jit(solution)/shard_map/all_gather | solution.py:442
  9.8 4.1 copy-start.9
  223.5 7.3 %copy-start.3 = (bf16[1024,1024]{1,0:T(8,128)(2,1)S(1)}, bf16[1024,1024]{1,0:T(8,128)(2,1)}, u32[]{:S(2)}) copy-start(bf16[1024,1024]{1,0:T(8,128)(2,1)} %to_home.1) | copy-start | bytes 6291460
  230.9 5.0 copy-start.12
  230.9 7.8 %copy-start.10 = (s32[1,16]{1,0:T(1,128)S(1)}, s32[1,16]{1,0:T(1,128)}, u32[]{:S(2)}) copy-start(s32[1,16]{1,0:T(1,128)} %param.15) | copy-start | bytes 196
  230.9 7.8 %copy-start.11 = (s32[1,16]{1,0:T(1,128)S(1)}, s32[1,16]{1,0:T(1,128)}, u32[]{:S(2)}) copy-start(s32[1,16]{1,0:T(1,128)} %param.16) | copy-start | bytes 196
  230.9 9.8 %copy-start.8 = (f32[2]{0:T(128)S(1)}, f32[2]{0:T(128)}, u32[]{:S(2)}) copy-start(f32[2]{0:T(128)} %constant.97.clone) | copy-start | bytes 28
  230.9 12.9 %copy-start.7 = (f32[4]{0:T(128)S(1)}, f32[4]{0:T(128)}, u32[]{:S(2)}) copy-start(f32[4]{0:T(128)} %constant.98.clone) | copy-start | bytes 52
  301.6 10.6 %copy-start.13 = (bf16[1024,1024]{1,0:T(8,128)(2,1)S(1)}, bf16[1024,1024]{1,0:T(8,128)(2,1)}, u32[]{:S(2)}) copy-start(bf16[1024,1024]{1,0:T(8,128)(2,1)} %fusion.51) | copy-start | bytes 6291460
  321.5 26.0 %copy-start.2 = (bf16[1024,640]{1,0:T(8,128)(2,1)S(1)}, bf16[1024,640]{1,0:T(8,128)(2,1)}, u32[]{:S(2)}) copy-start(bf16[1024,640]{1,0:T(8,128)(2,1)} %convolution_convert_fusion.g_in) | copy-start | bytes 3932164
  354.8 8.4 %copy-start.1 = (bf16[5,128,1024]{2,1,0:T(8,128)(2,1)S(1)}, bf16[5,128,1024]{2,1,0:T(8,128)(2,1)}, u32[]{:S(2)}) copy-start(bf16[5,128,1024]{2,1,0:T(8,128)(2,1)} %spread.1) | copy-start | bytes 3932164
  354.8 168.4 %copy-start.5 = (s32[2,8,5]{2,1,0:T(8,128)S(1)}, s32[2,8,5]{2,1,0:T(8,128)}, u32[]{:S(2)}) copy-start(s32[2,8,5]{2,1,0:T(8,128)} %constant.100.clone) | copy-start | bytes 964
  354.8 168.4 %copy-start.6 = (s32[2,8,5]{2,1,0:T(8,128)S(1)}, s32[2,8,5]{2,1,0:T(8,128)}, u32[]{:S(2)}) copy-start(s32[2,8,5]{2,1,0:T(8,128)} %constant.99.clone) | copy-start | bytes 964
  356.4 168.7 %all-to-all-start = ((bf16[16,512,128]{2,1,0:T(8,128)(2,1)}), bf16[16,512,128]{2,1,0:T(8,128)(2,1)S(1)}, u32[]{:S(2)}, u32[]{:S(2)}) async-start(bf16[16,512,128]{2,1,0:T(8,128)(2,1)} %select_select_fusion), calls=%async_computation | async-start | bytes 4194304 | tf_op jit(solution)/shard_map/all_to_all | solution.py:429
  572.5 5.4 copy-start
  593.9 4.1 copy-start.4
Sparse Core Ops, SparseCore 0:
  347.7 315.6 all-gather.1

commit v2 on v1

--- a/solution.py
+++ b/solution.py
@@ -7,6 +7,7 @@
 from jax.experimental import pallas as pl
 from jax.experimental.pallas import tpu as pltpu
 from jax.sharding import PartitionSpec as P
+
 
 BLK = 1024
 LANE = 128
@@ -234,23 +235,34 @@
     j = z // 2
     source = z * 2 + h
     dst = out.at[pl.ds(pl.multiple_of(h * half, half), half), pl.ds(pl.multiple_of(j * LANE, LANE), LANE)]
-    moves = []
-    for block in range(blocks):
-        row, col = block // cols, block % cols
-        home = lax.rem(home_of(block, blocks, n) + SHIFT * m, n)
-        src = g_in.at[pl.ds(row * half, half), pl.ds(col * LANE, LANE)]
-        mine = jnp.logical_and(home == z, h == m)
-        moves.append((
-            mine,
-            pltpu.make_async_copy(src, dst, recv.at[source]),
-            remote(src, dst, send.at[block], recv.at[source], dp=home, mp=m),
-        ))
-    for mine, local, far in moves:
-        @pl.when(mine)
-        def _():
-            local.start()
-
-        @pl.when(jnp.logical_not(mine))
+
+    def moves(o):
+        chip = lax.rem(z + o, n)
+        at = lax.rem(chip + n - SHIFT * m, n)
+        block = (at * blocks + n - 1) // n
+        used = jnp.logical_and(block < blocks, (n * block) // blocks == at)
+        src = g_in.at[
+            pl.ds(pl.multiple_of((block // cols) * half, half), half),
+            pl.ds(pl.multiple_of(lax.rem(block, cols) * LANE, LANE), LANE),
+        ]
+        local = pltpu.make_async_copy(src, dst, recv.at[source])
+        far = remote(src, dst, send.at[o], recv.at[source], dp=chip, mp=m)
+        mine = h == m if o == 0 else False
+        return used, mine, local, far
+
+    order = [n // 2]
+    for o in range(n // 2 - 1, 0, -1):
+        order.extend([o, n - o])
+    for o in order + [0]:
+        used, mine, local, far = moves(o)
+        if o == 0:
+            @pl.when(jnp.logical_and(used, mine))
+            def _():
+                local.start()
+
+            used = jnp.logical_and(used, jnp.logical_not(mine))
+
+        @pl.when(used)
         def _():
             far.start()
 
@@ -271,8 +283,12 @@
     def _():
         out[...] = jnp.zeros_like(out)
 
-    for mine, local, far in moves:
-        @pl.when(jnp.logical_not(mine))
+    for o in range(n):
+        used, mine, local, far = moves(o)
+        if o == 0:
+            used = jnp.logical_and(used, jnp.logical_not(mine))
+
+        @pl.when(used)
         def _():
             far.wait_send()
 
@@ -285,7 +301,7 @@
         out_shape=jax.ShapeDtypeStruct((BLK, BLK), jnp.bfloat16),
         in_specs=[vmem],
         out_specs=vmem,
-        scratch_shapes=[dma((rows * cols,)), dma((2 * n,))],
+        scratch_shapes=[dma((n,)), dma((2 * n,))],
         compiler_params=pltpu.CompilerParams(collective_id=2, has_side_effects=True),
         name="to_home",
     )(shard)
@@ -298,9 +314,9 @@
 MOVES = {
     0: ((5, -1, 2), (6, -1, 3), (7, -1, 4)),
     1: ((5, 1, 0), (6, 1, 1), (7, 1, 2)),
-    3: ((5, -1, 3), (6, -1, 4), (7, 2, 0)),
+    3: ((5, -1, 3), (7, -1, 4), (6, 2, 0)),
     4: ((5, 1, 1), (6, 1, 2), (7, 1, 3)),
-    6: ((5, -1, 4), (6, 1, 0), (7, 1, 1)),
+    6: ((7, -1, 4), (5, 1, 0), (6, 1, 1)),
 }
 
 
@@ -364,34 +380,77 @@
     return device, slot
 
 
-def place_kernel(cols, table, *refs):
-    scale_ref, out = refs[cols], refs[cols + 1]
+def place_early_kernel(cols, table, groups, *refs):
+    scale_ref, out = refs[cols], refs[-1]
     scale = scale_ref[0]
     for col in range(cols):
         wide = refs[col][0].astype(jnp.float32)
         out[:, col * BLK:(col + 1) * BLK] = (wide * scale).astype(jnp.bfloat16)
 
 
-def place(gathered, table, scale, rows, cols):
+def place_late_kernel(cols, early, late, choice, groups, *refs):
+    scale_ref, out = refs[2 * cols], refs[-1]
+    scale = scale_ref[0]
+    g = pl.program_id(0)
+    for col in range(cols):
+        for kind in range(2):
+            @pl.when(choice[g * cols + col] == kind)
+            def _(col=col, kind=kind):
+                wide = refs[kind * cols + col][0].astype(jnp.float32)
+                out[:, col * BLK:(col + 1) * BLK] = (wide * scale).astype(jnp.bfloat16)
+
+
+def place_early(gathered, table, groups, scale, rows, cols):
     high = BLK // PIECES
     picks = [
-        pl.BlockSpec((1, high, BLK), lambda g, tab, col=col: (tab[g * cols + col], 0, 0))
+        pl.BlockSpec((1, high, BLK), lambda g, tab, grp, col=col: (tab[g * cols + col], 0, 0))
         for col in range(cols)
     ]
     return pl.pallas_call(
-        functools.partial(place_kernel, cols),
+        functools.partial(place_early_kernel, cols),
         out_shape=jax.ShapeDtypeStruct((rows * BLK, cols * BLK), jnp.bfloat16),
         grid_spec=pltpu.PrefetchScalarGridSpec(
-            num_scalar_prefetch=1,
-            grid=(rows * PIECES,),
+            num_scalar_prefetch=2,
+            grid=(groups.shape[0],),
             in_specs=picks + [pl.BlockSpec(memory_space=pltpu.SMEM)],
-            out_specs=pl.BlockSpec((high, cols * BLK), lambda g, tab: (g, 0)),
+            out_specs=pl.BlockSpec((high, cols * BLK), lambda g, tab, grp: (grp[g], 0)),
         ),
-        name="place",
-    )(table, *([gathered] * cols), scale)
-
-
-def on_device(activations, out_grads, slot_table, exponent_index, damping_index):
+        cost_estimate=pl.CostEstimate(
+            flops=int(2e9), bytes_accessed=int(3e7), transcendentals=0
+        ),
+        name="place_early",
+    )(table, groups, *([gathered] * cols), scale)
+
+
+def place_late(gathered_early, gathered_late, early, late, choice, groups, scale, before, rows, cols):
+    high = BLK // PIECES
+    picks = [
+        pl.BlockSpec((1, high, BLK), lambda g, ta, tb, ch, grp, col=col: (ta[g * cols + col], 0, 0))
+        for col in range(cols)
+    ] + [
+        pl.BlockSpec((1, high, BLK), lambda g, ta, tb, ch, grp, col=col: (tb[g * cols + col], 0, 0))
+        for col in range(cols)
+    ]
+    return pl.pallas_call(
+        functools.partial(place_late_kernel, cols),
+        out_shape=jax.ShapeDtypeStruct((rows * BLK, cols * BLK), jnp.bfloat16),
+        grid_spec=pltpu.PrefetchScalarGridSpec(
+            num_scalar_prefetch=4,
+            grid=(groups.shape[0],),
+            in_specs=picks
+            + [pl.BlockSpec(memory_space=pltpu.SMEM), pl.BlockSpec(memory_space=pl.ANY)],
+            out_specs=pl.BlockSpec((high, cols * BLK), lambda g, ta, tb, ch, grp: (grp[g], 0)),
+        ),
+        input_output_aliases={4 + 2 * cols + 1: 0},
+        name="place_late",
+    )(early, late, choice, groups, *([gathered_early] * cols), *([gathered_late] * cols), scale, before)
+
+
+EARLY = (0, 1, 2, 3, 5, 6)
+LATE = (4, 7)
+
+
+def inner(activations, out_grads, slot_table, exponent_index, damping_index):
     n = lax.axis_size("dp")
     z = lax.axis_index("dp")
     h = lax.axis_index("mp")
@@ -439,7 +498,9 @@
     half_step = jnp.dot(left_root, home_grad, preferred_element_type=jnp.float32).astype(jnp.bfloat16)
     block_update = jnp.dot(half_step, right_root, preferred_element_type=jnp.float32).astype(jnp.bfloat16)
     dense = spread(block_update, n)
-    gathered = lax.all_gather(dense, "dp", axis=0, tiled=True)
+    first = KEEP - 1
+    gathered_early = lax.all_gather(dense[:first], "dp", axis=0, tiled=True)
+    gathered_late = lax.all_gather(dense[first:], "dp", axis=0, tiled=True)
 
     wide = dense.astype(jnp.float32)
     total_sq = lax.psum(jnp.sum(wide * wide), ("dp", "mp"))
@@ -455,8 +516,24 @@
     roots = jnp.stack(two_roots(slot_grad, exp_own, damp_own))
 
     device_tab, slot_tab = piece_tables(n, rows, cols)
-    table = lax.rem(jnp.asarray(device_tab) + SHIFT * h, n) * KEEP + jnp.asarray(slot_tab)
-    update = place(gathered, table.reshape(-1), rescale.reshape(1), rows, cols)
+    in_late = slot_tab == first
+
+    def tables_of(parts):
+        device_of = lax.rem(jnp.asarray(device_tab[:, parts].reshape(-1)) + SHIFT * h, n)
+        late = in_late[:, parts].reshape(-1)
+        early_at = jnp.where(late, 0, device_of * first + jnp.asarray(slot_tab[:, parts].reshape(-1)))
+        return early_at, jnp.where(late, device_of, 0), jnp.asarray(late.astype(np.int32))
+
+    def groups_of(parts):
+        return jnp.asarray([r * PIECES + i for r in range(rows) for i in parts], jnp.int32)
+
+    scale = rescale.reshape(1)
+    update = place_early(
+        gathered_early, tables_of(EARLY)[0], groups_of(EARLY), scale, rows, cols
+    )
+    update = place_late(
+        gathered_early, gathered_late, *tables_of(LATE), groups_of(LATE), scale, update, rows, cols
+    )
     return (update, roots[None, None])
 
 
@@ -469,7 +546,7 @@
         P(("member", "mp"), None),
     )
     return jax.shard_map(
-        on_device,
+        inner,
         mesh=mesh,
         in_specs=placed,
         out_specs=(P("member", "mp"), P(("member", "mp"), "dp", None, None, None)),

time: 700 us -> 707 us (1.010)
  the two profiles are of different devices: /device:TPU:69 before, /device:TPU:70 now
where the time goes in v2:
time: 707 us; the launch traced here: 699 us
  Pallas kernels  247 us (35%)
  blocking collectives  165 us (23%)
  matrix products  124 us (18%)
  waiting for transfers between devices  78.2 us (11%)
  other arithmetic  31.9 us (5%)
  between operations  25.3 us (4%)
  local copies, waits for them, and re-layouts  18.2 us (3%)
  starting transfers between devices  8.9 us (1%)
    psum x1, blocking collectives, inner(): total_sq = lax.psum(jnp.sum(wide * wide), ('dp', 'mp'))  159 us
    pallas_call x1, Pallas kernels, collect(): pl.pallas_call(functools.partial(collect_kernel, n), out_shape=(jax.Shape...  134 us
    dot_general x10, matrix products, half_dot(): jnp.dot(first.astype(jnp.bfloat16), second.astype(jnp.bfloat16), preferre...  74.9 us
    pallas_call x1, Pallas kernels, to_home(): pl.pallas_call(functools.partial(to_home_kernel, n, rows, cols), out_shap...  69.6 us
    all_gather x1, waiting for transfers between devices, inner(): gathered_late = lax.all_gather(dense[first:], 'dp', axis=0, tiled=True)  58.2 us
    pallas_call x1, Pallas kernels, spread(): pl.pallas_call(functools.partial(spread_kernel, n), out_shape=jax.ShapeDt...  20.6 us
    all_gather x1, waiting for transfers between devices, inner(): gathered_early = lax.all_gather(dense[:first], 'dp', axis=0, tiled=True)  20 us
    pallas_call x1, Pallas kernels, place_early(): pl.pallas_call(functools.partial(place_early_kernel, cols), out_shape=jax...  16.1 us
  transfers between devices with their start and end apart: 3, of which 2 were waited for; matrix products, arithmetic and copies ran while one was open for 11% of the time, Pallas kernels for 2%

profile of v2, /device:TPU:70, one launch (start us, length us, event | category | flops | bytes accessed | tf_op | source)
XLA Modules:
  0.0 698.5 jit_solution(3410484944670977490)
XLA Ops:
  14.5 133.5 %collect.1 = (bf16[16,128,1024]{2,1,0:T(8,128)(2,1)}, bf16[16,2,64,640]{3,2,1,0:T(8,128)(2,1)}, s32[8,128]{1,0:T(8,128)}) custom-call(bf16[128,1024]{1,0:T(8,128)(2,1)} %bitcast.90, bf16[8,128,640]{2,1,0:T(8,128)(2,1)} %copy.51.b_in, s32[8,128]{1,0:T(8,128)} %broadcast_in_dim.96.tbl_in), custom_call_target="tpu_custom_call" | custom-call | tf_op jit(solution)/shard_map/collect/pallas_call | solution.py:206
  148.1 7.6 %convolution_convert_fusion.g_in = bf16[1024,640]{1,0:T(8,128)(2,1)} fusion(bf16[2048,1024]{1,0:T(8,128)(2,1)} %bitcast.93, bf16[2048,640]{1,0:T(8,128)(2,1)} %bitcast.94), kind=kOutput, calls=%fused_computation.92 | convolution fusion | flops 2685009920 | bytes 8126464 | tf_op jit(solution)/shard_map/dot_general | solution.py:473
  155.7 69.6 %to_home.1 = bf16[1024,1024]{1,0:T(8,128)(2,1)} custom-call(bf16[1024,640]{1,0:T(8,128)(2,1)} %convolution_convert_fusion.g_in), custom_call_target="tpu_custom_call" | custom-call | tf_op jit(solution)/shard_map/to_home/pallas_call | solution.py:299
  225.2 7.4 %select_reduce_fusion.7 = (f32[]{:T(128)}, f32[1024,1024]{1,0:T(8,128)}) fusion(bf16[1024,1024]{1,0:T(8,128)(2,1)} %to_home.1), kind=kOutput, calls=%fused_computation.41 | convolution fusion | flops 2150629376 | bytes 6291460 | tf_op jit(solution)/shard_map/dot_general | solution.py:52
  232.6 5.0 select_reduce_fusion.5
  251.2 7.8 %fusion.106 = bf16[1024,1024]{1,0:T(8,128)(2,1)} fusion(f32[1024,1024]{1,0:T(8,128)} %get-tuple-element.27, f32[]{:T(128)} %get-tuple-element.13, f32[]{:T(128)S(6)} %div.64, f32[]{:T(128)S(6)} %mul.117, f32[]{:T(128)S(6)} %add.83), kind=kOutput, calls=%fused_computation.141 | convolution fusion | flops 2155872256 | bytes 6291472 | tf_op jit(solution)/shard_map/dot_general | solution.py:27
  259.1 10.5 %fusion.3 = bf16[1024,1024]{1,0:T(8,128)(2,1)} fusion(f32[1024,1024]{1,0:T(8,128)} %get-tuple-element.27, bf16[1024,1024]{1,0:T(8,128)(2,1)} %fusion.106, f32[]{:T(128)} %get-tuple-element.13, f32[]{:T(128)S(6)} %div.64, f32[]{:T(128)S(6)} %mul.117, f32[]{:T(128)S(6)} %add.83, pred[]{:T(512)S(6)} %eq.126), kind=kOutput, calls=%fused_computation.12 | convolution fusion | flops 4306501632 | bytes 8388625 | tf_op jit(solution)/shard_map/dot_general | solution.py:27
  269.6 9.5 %fusion.51 = bf16[1024,1024]{1,0:T(8,128)(2,1)} fusion(bf16[1024,1024]{1,0:T(8,128)(2,1)S(1)} %copy-done.3, bf16[1024,1024]{1,0:T(8,128)(2,1)} %fusion.3, f32[1024,1024]{1,0:T(8,128)} %get-tuple-element.27, f32[]{:T(128)} %get-tuple-element.13, f32[]{:T(128)S(6)} %div.64, f32[]{:T(128)S(6)} %mul.117, f32[]{:T(128)S(6)} %add.83), kind=kOutput, calls=%fused_computation.75 | convolution fusion | flops 4304404480 | bytes 10485776 | tf_op jit(solution)/shard_map/dot_general | solution.py:498
  280.4 2.9 select_reduce_fusion.4
  284.0 7.8 %fusion.102 = bf16[1024,1024]{1,0:T(8,128)(2,1)} fusion(f32[1024,1024]{1,0:T(8,128)} %get-tuple-element.29, f32[]{:T(128)S(6)} %div.69, f32[]{:T(128)S(6)} %mul.123, f32[]{:T(128)} %get-tuple-element.13, f32[]{:T(128)S(6)} %add.83), kind=kOutput, calls=%fused_computation.140 | convolution fusion | flops 2155872256 | bytes 6291472 | tf_op jit(solution)/shard_map/dot_general | solution.py:27
  291.8 10.6 %fusion.7 = bf16[1024,1024]{1,0:T(8,128)(2,1)} fusion(f32[1024,1024]{1,0:T(8,128)} %get-tuple-element.29, bf16[1024,1024]{1,0:T(8,128)(2,1)} %fusion.102, f32[]{:T(128)S(6)} %div.69, f32[]{:T(128)S(6)} %mul.123, f32[]{:T(128)} %get-tuple-element.13, f32[]{:T(128)S(6)} %add.83, pred[]{:T(512)S(6)} %eq.126), kind=kOutput, calls=%fused_computation.16 | convolution fusion | flops 4306501632 | bytes 8388625 | tf_op jit(solution)/shard_map/dot_general | solution.py:27
  302.4 9.3 %fusion.69.upd = bf16[1024,1024]{1,0:T(8,128)(2,1)} fusion(bf16[1024,1024]{1,0:T(8,128)(2,1)S(1)} %copy-done.16, bf16[1024,1024]{1,0:T(8,128)(2,1)} %fusion.7, f32[1024,1024]{1,0:T(8,128)} %get-tuple-element.29, f32[]{:T(128)S(6)} %div.69, f32[]{:T(128)S(6)} %mul.123, f32[]{:T(128)} %get-tuple-element.13, f32[]{:T(128)S(6)} %add.83), kind=kOutput, calls=%fused_computation.89 | convolution fusion | flops 4305453056 | bytes 10485776 | tf_op jit(solution)/shard_map/dot_general | solution.py:499
  311.8 20.6 %spread.1 = bf16[5,128,1024]{2,1,0:T(8,128)(2,1)} custom-call(bf16[1024,1024]{1,0:T(8,128)(2,1)} %fusion.69.upd), custom_call_target="tpu_custom_call" | custom-call | tf_op jit(solution)/shard_map/spread/pallas_call | solution.py:356
  337.2 3.5 copy.53
  343.6 8.8 %all-to-all-start = ((bf16[16,512,128]{2,1,0:T(8,128)(2,1)}), bf16[16,512,128]{2,1,0:T(8,128)(2,1)S(1)}, u32[]{:S(2)}, u32[]{:S(2)}) async-start(bf16[16,512,128]{2,1,0:T(8,128)(2,1)} %select_select_fusion), calls=%async_computation | async-start | bytes 4194304 | tf_op jit(solution)/shard_map/all_to_all | solution.py:488
  354.5 159.4 %psum.7 = f32[]{:T(128)} all-reduce(f32[]{:T(128)} %multiply_reduce_fusion), channel_id=1, replica_groups=mesh['member'=4,'dp'=16,'mp'=2] {'dp','mp'}, use_global_device_ids=true, to_apply=%region_11.12 | all-reduce | flops 1 | bytes 8 | tf_op jit(solution)/shard_map/psum | solution.py:506
  518.8 5.4 all_to_all.10
  524.3 5.0 select_reduce_fusion.1
  530.5 3.0 select_reduce_fusion
  534.2 5.0 select_reduce_fusion.3
  540.5 3.0 select_reduce_fusion.2
  544.1 3.6 fusion.13
  547.6 3.7 fusion.110
  551.3 10.6 %fusion.15 = bf16[1024,1024]{1,0:T(8,128)(2,1)} fusion(f32[1024,1024]{1,0:T(8,128)} %get-tuple-element.31, bf16[1024,1024]{1,0:T(8,128)(2,1)} %fusion.110, f32[]{:T(128)S(6)} %div.79, f32[]{:T(128)S(6)} %mul.140, f32[]{:T(128)} %get-tuple-element.12, f32[]{:T(128)S(6)} %add.92, pred[]{:T(512)S(6)} %eq.137), kind=kOutput, calls=%fused_computation.24 | convolution fusion | flops 4306501632 | bytes 8388625 | tf_op jit(solution)/shard_map/dot_general | solution.py:27
  561.9 5.4 convert_bitcast_fusion
  568.8 3.7 fusion.109
  572.5 10.6 %fusion.11 = bf16[1024,1024]{1,0:T(8,128)(2,1)} fusion(f32[1024,1024]{1,0:T(8,128)} %get-tuple-element.33, bf16[1024,1024]{1,0:T(8,128)(2,1)} %fusion.109, f32[]{:T(128)} %get-tuple-element.12, f32[]{:T(128)S(6)} %div.74, f32[]{:T(128)S(6)} %mul.134, f32[]{:T(128)S(6)} %add.92, pred[]{:T(512)S(6)} %eq.137), kind=kOutput, calls=%fused_computation.20 | convolution fusion | flops 4306501632 | bytes 8388625 | tf_op jit(solution)/shard_map/dot_general | solution.py:27
  583.1 4.1 convert_bitcast_fusion.1
  589.6 20.0 %all-gather.3.cloned.1.call-done.refs_0_.refs_1_.refs_2_.refs_3_.refs_4_ = bf16[64,128,1024]{2,1,0:T(8,128)(2,1)} async-done(((bf16[4,128,1024]{2,1,0:T(8,128)(2,1)}), bf16[64,128,1024]{2,1,0:T(8,128)(2,1)}) %all-gather.3.cloned.1.call-update) | async-done | bytes 16777232 | tf_op jit(solution)/shard_map/all_gather | solution.py:502
  609.5 16.1 %place_early.1.refs_11_ = bf16[2048,5120]{1,0:T(8,128)(2,1)} custom-call(s32[60]{0:T(128)} %fusion.84.table, s32[12]{0:T(128)} %constant.119.clone.groups, bf16[64,128,1024]{2,1,0:T(8,128)(2,1)} %all-gather.3.cloned.1.call-done.refs_0_.refs_1_.refs_2_.refs_3_.refs_4_, ...), custom_call_target="tpu_custom_call" | custom-call | flops 2000000000 | bytes 30000000 | tf_op jit(solution)/shard_map/place_early/pallas_call | solution.py:409
  625.6 58.2 %all-gather.5.cloned.1.call-done.refs_5_.refs_6_.refs_7_.refs_8_.refs_9_ = bf16[16,128,1024]{2,1,0:T(8,128)(2,1)} async-done(((bf16[1,128,1024]{2,1,0:T(8,128)(2,1)}), bf16[16,128,1024]{2,1,0:T(8,128)(2,1)}) %all-gather.5.cloned.1.call-update) | async-done | bytes 4194320 | tf_op jit(solution)/shard_map/all_gather | solution.py:503
  683.8 7.7 %place_late.1 = bf16[2048,5120]{1,0:T(8,128)(2,1)} custom-call(s32[20]{0:T(128)} %add_select_fusion.early, s32[20]{0:T(128)} %get-tuple-element.20.late, s32[20]{0:T(128)} %constant.123.clone.choice, s32[4]{0:T(128)} %constant.124.clone.groups, ...), custom_call_target="tpu_custom_call", output_to_operand_aliasing={{}: (15, {})} | custom-call | tf_op jit(solution)/shard_map/place_late/pallas_call | solution.py:434
  (72 shorter events, 34.4 us)
Async XLA Ops:
  7.2 602.4 %all-gather.3.cloned.1.call-start = ((), (), s32[]{:S(2)}) async-start(), calls=%async_computation.2 | async-start | bytes 17825792 | tf_op jit(solution)/shard_map/all_gather | solution.py:502
  9.8 4.1 copy-start.9
  225.2 7.4 %copy-start.3 = (bf16[1024,1024]{1,0:T(8,128)(2,1)S(1)}, bf16[1024,1024]{1,0:T(8,128)(2,1)}, u32[]{:S(2)}) copy-start(bf16[1024,1024]{1,0:T(8,128)(2,1)} %to_home.1) | copy-start | bytes 6291460
  232.6 5.0 copy-start.15
  232.6 7.6 %copy-start.13 = (s32[1,16]{1,0:T(1,128)S(1)}, s32[1,16]{1,0:T(1,128)}, u32[]{:S(2)}) copy-start(s32[1,16]{1,0:T(1,128)} %param.22) | copy-start | bytes 196
  232.6 7.6 %copy-start.14 = (s32[1,16]{1,0:T(1,128)S(1)}, s32[1,16]{1,0:T(1,128)}, u32[]{:S(2)}) copy-start(s32[1,16]{1,0:T(1,128)} %param.23) | copy-start | bytes 196
  232.6 9.5 %copy-start.8 = (f32[2]{0:T(128)S(1)}, f32[2]{0:T(128)}, u32[]{:S(2)}) copy-start(f32[2]{0:T(128)} %constant.114.clone) | copy-start | bytes 28
  232.6 12.6 %copy-start.7 = (f32[4]{0:T(128)S(1)}, f32[4]{0:T(128)}, u32[]{:S(2)}) copy-start(f32[4]{0:T(128)} %constant.115.clone) | copy-start | bytes 52
  291.8 10.6 %copy-start.16 = (bf16[1024,1024]{1,0:T(8,128)(2,1)S(1)}, bf16[1024,1024]{1,0:T(8,128)(2,1)}, u32[]{:S(2)}) copy-start(bf16[1024,1024]{1,0:T(8,128)(2,1)} %fusion.51) | copy-start | bytes 6291460
  311.8 23.0 %copy-start.2 = (bf16[1024,640]{1,0:T(8,128)(2,1)S(1)}, bf16[1024,640]{1,0:T(8,128)(2,1)}, u32[]{:S(2)}) copy-start(bf16[1024,640]{1,0:T(8,128)(2,1)} %convolution_convert_fusion.g_in) | copy-start | bytes 3932164
  341.9 10.5 %copy-start.1 = (bf16[5,128,1024]{2,1,0:T(8,128)(2,1)S(1)}, bf16[5,128,1024]{2,1,0:T(8,128)(2,1)}, u32[]{:S(2)}) copy-start(bf16[5,128,1024]{2,1,0:T(8,128)(2,1)} %spread.1) | copy-start | bytes 3932164
  343.6 172.3 %copy-start.11 = (s32[60]{0:T(128)S(1)}, s32[60]{0:T(128)}, u32[]{:S(2)}) copy-start(s32[60]{0:T(128)} %constant.117.clone) | copy-start | bytes 724
  343.6 172.3 %copy-start.12 = (s32[60]{0:T(128)S(1)}, s32[60]{0:T(128)}, u32[]{:S(2)}) copy-start(s32[60]{0:T(128)} %constant.116.clone) | copy-start | bytes 724
  343.6 172.9 %copy-start.5 = (pred[20]{0:T(512)(128)(4,1)S(1)}, pred[20]{0:T(512)(128)(4,1)}, u32[]{:S(2)}) copy-start(pred[20]{0:T(512)(128)(4,1)} %constant.122.clone) | copy-start | bytes 64
  343.6 172.9 %copy-start.6 = (s32[20]{0:T(128)S(1)}, s32[20]{0:T(128)}, u32[]{:S(2)}) copy-start(s32[20]{0:T(128)} %constant.120.clone) | copy-start | bytes 244
  343.6 173.4 %copy-start.10 = (s32[20]{0:T(128)S(1)}, s32[20]{0:T(128)}, u32[]{:S(2)}) copy-start(s32[20]{0:T(128)} %constant.121.clone) | copy-start | bytes 244
  343.6 173.9 %all-to-all-start = ((bf16[16,512,128]{2,1,0:T(8,128)(2,1)}), bf16[16,512,128]{2,1,0:T(8,128)(2,1)S(1)}, u32[]{:S(2)}, u32[]{:S(2)}) async-start(bf16[16,512,128]{2,1,0:T(8,128)(2,1)} %select_select_fusion), calls=%async_computation | async-start | bytes 4194304 | tf_op jit(solution)/shard_map/all_to_all | solution.py:488
  352.4 331.4 %all-gather.5.cloned.1.call-start = ((), (), s32[]{:S(2)}) async-start(), calls=%async_computation.3 | async-start | bytes 4456448 | tf_op jit(solution)/shard_map/all_gather | solution.py:503
  561.9 5.4 copy-start
  583.1 4.1 copy-start.4
Sparse Core Ops, SparseCore 0:
  334.9 274.6 all-gather.2
  611.2 72.5 all-gather.4

commit v3 on v0

v3 whole, which is shorter than its diff:
```python
import functools

import jax
import jax.numpy as jnp
import numpy as np
from jax import lax
from jax.experimental import pallas as pl
from jax.experimental.pallas import tpu as pltpu
from jax.sharding import PartitionSpec as P

BLK = 1024
LANE = 128
ROOT_ORDERS = (2.0, 4.0)
DAMPINGS = (0.03, 0.1, 0.3, 1.0)
SHIFT = 4
MESH = pl.DeviceIdType.MESH


STRIPE = 256


def eye_stripe(at, size):
    row = lax.broadcasted_iota(jnp.int32, (STRIPE, size), 0) + at
    col = lax.broadcasted_iota(jnp.int32, (STRIPE, size), 1)
    return row == col


def dot32(first, second, dims=((1,), (0,))):
    return lax.dot_general(first, second, (dims, ((), ())), preferred_element_type=jnp.float32)


def over_stripes(size, body):
    def step(index, carry):
        body(pl.multiple_of(index * STRIPE, STRIPE))
        return carry

    lax.fori_loop(0, size // STRIPE, step, 0)


def root_into(g, root, order, quartic, damping, trace, gt, m0, t0, q, r, only=None):
    size = g.shape[0]
    shift = damping * (trace / size + 1.0)
    ratio = size / (2.0 * (trace + shift * size))
    base = g if gt is None else gt

    def stat(at):
        rows = pl.ds(at, STRIPE)
        s = dot32(base[rows, :], base[...], ((1,), (1,)))
        on = eye_stripe(at, size)
        scaled = jnp.where(on, s + shift, s) * ratio
        m0[rows, :] = scaled.astype(jnp.bfloat16)
        t0[rows, :] = (jnp.where(on, (order + 1.0) - scaled, -scaled) / order).astype(jnp.bfloat16)

    def square(at):
        rows = pl.ds(at, STRIPE)
        q[rows, :] = dot32(t0[rows, :], t0[...]).astype(jnp.bfloat16)

    def fourth(at):
        rows = pl.ds(at, STRIPE)
        f = dot32(q[rows, :], q[...])
        r[rows, :] = jnp.where(quartic, f, q[rows, :].astype(jnp.float32)).astype(jnp.bfloat16)

    def factor(at):
        rows = pl.ds(at, STRIPE)
        m = dot32(r[rows, :], m0[...])
        on = eye_stripe(at, size)
        q[rows, :] = (jnp.where(on, (order + 1.0) - m, -m) / order).astype(jnp.bfloat16)

    def last(at):
        rows = pl.ds(at, STRIPE)
        root[rows, :] = dot32(t0[rows, :], q[...]).astype(jnp.bfloat16)

    for index, body in enumerate((stat, square, fourth, factor, last)):
        if only is None or only == index:
            over_stripes(size, body)


def trace_and_turn(g, gt, acc):
    size = g.shape[0]
    acc[...] = jnp.zeros_like(acc)

    def body(at):
        rows = pl.ds(at, STRIPE)
        part = g[rows, :]
        wide = part.astype(jnp.float32)
        acc[...] += jnp.sum((wide * wide).reshape(STRIPE // 8, 8, size), axis=0)
        gt[:, rows] = part.T

    over_stripes(size, body)
    return jnp.sum(acc[...])


def picks_of(codes):
    quartic = codes[0] == 1
    order = jnp.where(quartic, ROOT_ORDERS[1], ROOT_ORDERS[0])
    damping = jnp.float32(DAMPINGS[0])
    for index in range(1, len(DAMPINGS)):
        damping = jnp.where(codes[1] == index, jnp.float32(DAMPINGS[index]), damping)
    return quartic, order, damping


def greet_group(n, z, h):
    barrier = pltpu.get_barrier_semaphore()
    pl.semaphore_signal(barrier, inc=1, device_id={"mp": 1 - h}, device_id_type=MESH)
    for o in range(1, n):
        for t in range(2):
            pl.semaphore_signal(
                barrier, inc=1, device_id={"dp": lax.rem(z + o, n), "mp": t}, device_id_type=MESH
            )
    pl.semaphore_wait(barrier, 2 * n - 1)


def remote(src, dst, send, recv, **to):
    return pltpu.make_async_remote_copy(
        src_ref=src, dst_ref=dst, send_sem=send, recv_sem=recv, device_id=to, device_id_type=MESH
    )


def landed(ref, sem):
    pltpu.make_async_copy(ref, ref, sem).wait()


def both_ways(n):
    order = [n // 2]
    for o in range(n // 2 - 1, 0, -1):
        order.extend([o, n - o])
    return order + [0]


QUARTERS = 4


def step_kernel(
    n, rows, cols,
    codes, table_own, a_in, b_in, table_in,
    raw, roots, parts,
    a_all, b_all, table_far, table_smem, acc, shard, payload, home_g, slot_g, upd, part_out,
    gt, m0, t0, q, r, lane_acc,
    as_r, ar_r, as_l, ar_l, b_send, b_recv, f_send, f_recv, t_send, t_recv, loc,
    h_send, h_recv, s_send, s_recv, p_send, p_recv, gs_r, gr_r, gs_l, gr_l,
):
    z = lax.axis_index("dp")
    h = lax.axis_index("mp")
    blocks = rows * cols
    width, tok = a_in.shape
    half_tok = tok // 2
    half = BLK // 2
    right, left = lax.rem(z + 1, n), lax.rem(z + n - 1, n)
    steps = n // 2
    greet_group(n, z, h)

    top, low = pl.ds(0, width // 2), pl.ds(width // 2, width // 2)
    ring = []

    def ring_send(step):
        if step == 0:
            src_r = src_l = a_in
            at_r = at_l = z
        else:
            at_r = lax.rem(z + n - step, n)
            at_l = lax.rem(z + step, n)
            src_r, src_l = a_all.at[at_r], a_all.at[at_l]
        dst_r, dst_l = a_all.at[at_r], a_all.at[at_l]
        if step == steps - 1:
            src_r, dst_r = src_r.at[top], dst_r.at[top]
            src_l, dst_l = src_l.at[low], dst_l.at[low]
        one = remote(src_r, dst_r, as_r.at[step], ar_r.at[step], dp=right)
        two = remote(src_l, dst_l, as_l.at[step], ar_l.at[step], dp=left)
        one.start()
        two.start()
        ring.extend([one, two])

    def ring_recv(step):
        dst_r = a_all.at[lax.rem(z + n - step - 1, n)]
        dst_l = a_all.at[lax.rem(z + step + 1, n)]
        if step == steps - 1:
            dst_r, dst_l = dst_r.at[top], dst_l.at[low]
        landed(dst_r, ar_r.at[step])
        landed(dst_l, ar_l.at[step])

    table = remote(table_in, table_far, t_send, t_recv, mp=1 - h)
    table.start()
    own_a = pltpu.make_async_copy(a_in, a_all.at[z], loc.at[0])
    own_a.start()
    ring_send(0)
    parity = lax.rem(z + h, 2)
    h_rows = pl.ds(pl.multiple_of(h * half_tok, half_tok), half_tok)
    o_rows = pl.ds(pl.multiple_of((1 - h) * half_tok, half_tok), half_tok)

    def piece(i):
        chip = lax.rem(z + parity + 2 * i, n)
        block = b_in.at[chip // 2]
        same = remote(block.at[h_rows], b_all.at[z, h], b_send.at[i, 0], b_recv.at[z], dp=chip, mp=h)
        other = remote(
            block.at[o_rows], b_all.at[z, 1 - h], b_send.at[i, 1], b_recv.at[z], dp=chip, mp=1 - h
        )
        return same, other

    self_chip = parity == 0
    order = []
    for i in range(n // 4):
        order.extend([i, n // 2 - 1 - i])
    for i in order:
        same, other = piece(i)
        if i == 0:
            @pl.when(self_chip)
            def _():
                pltpu.make_async_copy(
                    b_in.at[z // 2].at[h_rows], b_all.at[z, h], b_recv.at[z]
                ).start()

            @pl.when(jnp.logical_not(self_chip))
            def _():
                same.start()
        else:
            same.start()
        other.start()

    def forward(at):
        landed(b_all.at[at, h], b_recv.at[at])
        remote(b_all.at[at, h], b_all.at[at, h], f_send.at[at], f_recv.at[at], mp=1 - h).start()

    def add_source(at, fresh=False):
        landed(b_all.at[at, 1 - h], f_recv.at[at])

        def body(low_row):
            span = pl.ds(low_row, STRIPE)
            got = dot32(a_all[at, span, :], b_all[at].reshape(tok, cols * LANE))
            if fresh:
                acc[span, :] = got
            else:
                acc[span, :] += got

        over_stripes(width, body)

    forward(z)
    own_a.wait()
    for step in range(steps):
        ring_recv(step)
        if step < steps - 1:
            ring_send(step + 1)
        if step == steps - 1:
            forward(lax.rem(z + steps, n))
        else:
            forward(lax.rem(z + step + 1, n))
            forward(lax.rem(z + n - step - 1, n))
        if step == 0:
            add_source(z, True)
        else:
            add_source(lax.rem(z + step, n))
            add_source(lax.rem(z + n - step, n))
    add_source(lax.rem(z + steps, n))
    for row in range(rows):
        for col in range(cols):
            shard[row * cols + col] = acc[
                row * half:(row + 1) * half, col * LANE:(col + 1) * LANE
            ].astype(jnp.bfloat16)

    m = lax.rem(z, 2)
    j = z // 2
    source = z * 2 + h
    spot_of = lambda chip, side: lax.rem(chip + n - SHIFT * side, n)
    my_rows = pl.ds(pl.multiple_of(h * half, half), half)
    my_cols = pl.ds(pl.multiple_of(j * LANE, LANE), LANE)

    def home_move(o):
        chip = lax.rem(z + o, n)
        at = spot_of(chip, m)
        block = (at * blocks + n - 1) // n
        used = jnp.logical_and(block < blocks, (n * block) // blocks == at)
        block = jnp.minimum(block, blocks - 1)
        dst = home_g.at[my_rows, my_cols]
        far = remote(shard.at[block], dst, h_send.at[o], h_recv.at[source], dp=chip, mp=m)
        return used, block, dst, far

    def home_go(o, start):
        used, block, dst, far = home_move(o)
        if o == 0:
            if start:
                @pl.when(jnp.logical_and(used, h == m))
                def _():
                    pltpu.make_async_copy(shard.at[block], dst, h_recv.at[source]).start()

            used = jnp.logical_and(used, h != m)

        @pl.when(used)
        def _():
            if start:
                far.start()
            else:
                far.wait_send()

    for o in both_ways(n):
        home_go(o, True)

    table.wait()
    to_smem = pltpu.make_async_copy(table_far, table_smem, loc.at[1])
    to_smem.start()
    to_smem.wait()

    def slot_move(o):
        chip = lax.rem(z + o, n)
        dst = slot_g.at[my_rows, my_cols]
        return chip, dst, remote(payload.at[chip], dst, s_send.at[o], s_recv.at[source], dp=chip, mp=m)

    for slot in range(n):
        pick = jnp.int32(0)
        filled = jnp.int32(0)
        for block in range(blocks):
            served = jnp.where(m == h, table_own[0, block], table_smem[0, block])
            pick = jnp.where(served == slot, block, pick)
            filled = jnp.where(served == slot, 1, filled)
        part = shard[pick]
        payload[slot] = jnp.where(filled == 1, part, jnp.zeros_like(part))
    for o in both_ways(n):
        chip, dst, far = slot_move(o)
        if o == 0:
            @pl.when(h == m)
            def _():
                pltpu.make_async_copy(payload.at[chip], dst, s_recv.at[source]).start()

            @pl.when(h != m)
            def _():
                far.start()
        else:
            far.start()

    spot = spot_of(z, h)
    own_block = (spot * blocks + n - 1) // n
    busy = jnp.logical_and(own_block < blocks, (n * own_block) // blocks == spot)
    lane_acc[...] = jnp.zeros_like(lane_acc)

    def all_pieces(ref, sems):
        for jj in range(n // 2):
            for t in range(2):
                landed(
                    ref.at[pl.ds(t * half, half), pl.ds(jj * LANE, LANE)],
                    sems.at[(2 * jj + h) * 2 + t],
                )

    def place_of(block, quarter):
        high = BLK // QUARTERS
        return raw.at[
            pl.ds(pl.multiple_of((block // cols) * BLK + quarter * high, high), high),
            pl.ds(pl.multiple_of(lax.rem(block, cols) * BLK, BLK), BLK),
        ]

    def quarter_of(quarter):
        high = BLK // QUARTERS
        return upd.at[pl.ds(quarter * high, high)]

    def own_moves(quarter):
        block = jnp.minimum(own_block, blocks - 1)
        src, dst = quarter_of(quarter), place_of(block, quarter)
        return (
            remote(src, dst, gs_r.at[block, quarter], gr_r.at[block, quarter], dp=right),
            remote(src, dst, gs_l.at[block, quarter], gr_l.at[block, quarter], dp=left),
            pltpu.make_async_copy(src, dst, loc.at[2 + quarter]),
        )

    @pl.when(busy)
    def _():
        all_pieces(home_g, h_recv)
        quartic, order_p, damping = picks_of([codes[0], codes[1]])
        trace = trace_and_turn(home_g, gt, lane_acc)
        root_into(home_g, roots.at[0], order_p, quartic, damping, trace, None, m0, t0, q, r)
        root_into(home_g, roots.at[1], order_p, quartic, damping, trace, gt, m0, t0, q, r)

        def halve(at):
            span = pl.ds(at, STRIPE)
            q[span, :] = dot32(roots[0, span, :], home_g[...]).astype(jnp.bfloat16)

        over_stripes(BLK, halve)
        lane_acc[...] = jnp.zeros_like(lane_acc)

        def finish(at):
            span = pl.ds(at, STRIPE)
            block = dot32(q[span, :], roots[1]).astype(jnp.bfloat16)
            upd[span, :] = block
            wide = block.astype(jnp.float32)
            lane_acc[...] += jnp.sum((wide * wide).reshape(STRIPE // 8, 8, BLK), axis=0)

        over_stripes(BLK, finish)
        for quarter in range(QUARTERS):
            for one in own_moves(quarter):
                one.start()

    tile = lane_acc[:, :LANE]
    for part in range(1, BLK // LANE):
        tile = tile + lane_acc[:, part * LANE:(part + 1) * LANE]
    part_out[...] = tile
    parts[source] = tile

    hop_right, hop_left = n // 2, n - 1 - n // 2

    def right_block(i):
        x = lax.rem(spot + n - 1, n)
        block = lax.rem(((x + 1) * blocks - 1) // n + blocks - i, blocks)
        return block, lax.rem(spot + n - (n * block) // blocks, n)

    def left_block(i):
        block = lax.rem(((spot + 1) * blocks - 1) // n + 1 + i, blocks)
        return block, lax.rem((n * block) // blocks + n - spot, n)

    def stream(i, quarter, side, phase):
        block, far = (right_block if side == 0 else left_block)(i)
        limit = hop_right if side == 0 else hop_left
        recv = (gr_r if side == 0 else gr_l).at[block, quarter]
        send = (gs_r if side == 0 else gs_l).at[block, quarter]
        ref = place_of(block, quarter)
        go = remote(ref, ref, send, recv, dp=right if side == 0 else left)
        if phase == 0:
            @pl.when(far < limit)
            def _():
                landed(ref, recv)
                go.start()
        elif phase == 1:
            @pl.when(far == limit)
            def _():
                landed(ref, recv)
        else:
            @pl.when(far < limit)
            def _():
                go.wait_send()

    slot_vals = {}

    def slot_first():
        all_pieces(slot_g, s_recv)
        slot_vals["picks"] = picks_of([codes[2], codes[3]])
        slot_vals["trace"] = trace_and_turn(slot_g, gt, lane_acc)

    def slot_unit(side, body):
        def run():
            quartic, order_p, damping = slot_vals["picks"]
            root_into(
                slot_g, roots.at[side], order_p, quartic, damping, slot_vals["trace"],
                None if side == 0 else gt, m0, t0, q, r, only=body,
            )
        return run

    units = [slot_first] + [slot_unit(side, body) for side in range(2) for body in range(5)]

    def part_move(o, t):
        return remote(
            part_out, parts.at[source], p_send.at[o, t], p_recv.at[source],
            dp=lax.rem(z + o, n), mp=t,
        )

    def part_each(act):
        remote_self = remote(
            part_out, parts.at[source], p_send.at[0, 0], p_recv.at[source], mp=1 - h
        )
        act(remote_self)
        for o in range(1, n):
            for t in range(2):
                act(part_move(o, t))

    most = (blocks + 1) // 2
    for i in range(most):
        for quarter in range(QUARTERS):
            stream(i, quarter, 0, 0)
            stream(i, quarter, 1, 0)
            if i == 0 and quarter == 0:
                part_each(lambda go: go.start())
            if i > 0 and units:
                units.pop(0)()
    for unit in units:
        unit()
    for i in range(most):
        for quarter in range(QUARTERS):
            stream(i, quarter, 0, 1)
            stream(i, quarter, 1, 1)

    for o in range(1, n):
        chip = lax.rem(z + o, n)
        for t in range(2):
            landed(parts.at[chip * 2 + t], p_recv.at[chip * 2 + t])
    landed(parts.at[z * 2 + 1 - h], p_recv.at[z * 2 + 1 - h])
    part_each(lambda go: go.wait_send())
    for one in ring:
        one.wait_send()
    for i in range(n // 2):
        same, other = piece(i)
        if i == 0:
            @pl.when(jnp.logical_not(self_chip))
            def _():
                same.wait_send()
        else:
            same.wait_send()
        other.wait_send()
    for o in range(n):
        at = lax.rem(z + o, n)
        remote(b_all.at[at, h], b_all.at[at, h], f_send.at[at], f_recv.at[at], mp=1 - h).wait_send()
        home_go(o, False)
        chip, dst, far = slot_move(o)
        if o == 0:
            @pl.when(h != m)
            def _():
                far.wait_send()
        else:
            far.wait_send()

    @pl.when(busy)
    def _():
        for quarter in range(QUARTERS):
            one, two, local = own_moves(quarter)
            one.wait_send()
            two.wait_send()
            local.wait()

    for i in range(most):
        for quarter in range(QUARTERS):
            stream(i, quarter, 0, 2)
            stream(i, quarter, 1, 2)


def run_step(codes, table_own, a_part, b_part, table, n, rows, cols):
    width, tok = a_part.shape
    dma = pltpu.SemaphoreType.DMA
    smem = pl.BlockSpec(memory_space=pltpu.SMEM)
    vmem = pl.BlockSpec(memory_space=pltpu.VMEM)
    blocks = rows * cols
    half = BLK // 2
    bf = lambda *shape: pltpu.VMEM(shape, jnp.bfloat16)
    steps = n // 2
    return pl.pallas_call(
        functools.partial(step_kernel, n, rows, cols),
        out_shape=(
            jax.ShapeDtypeStruct((rows * BLK, cols * BLK), jnp.bfloat16),
            jax.ShapeDtypeStruct((2, BLK, BLK), jnp.bfloat16),
            jax.ShapeDtypeStruct((2 * n, 8, LANE), jnp.float32),
        ),
        in_specs=[smem, smem, vmem, vmem, vmem],
        out_specs=(pl.BlockSpec(memory_space=pl.ANY), vmem, vmem),
        scratch_shapes=[
            bf(n, width, tok), bf(n, 2, tok // 2, cols * LANE),
            pltpu.VMEM((8, LANE), jnp.int32), pltpu.SMEM((8, LANE), jnp.int32),
            pltpu.VMEM((width, cols * LANE), jnp.float32),
            bf(blocks, half, LANE), bf(n, half, LANE), bf(BLK, BLK), bf(BLK, BLK), bf(BLK, BLK),
            pltpu.VMEM((8, LANE), jnp.float32),
            bf(BLK, BLK), bf(BLK, BLK), bf(BLK, BLK), bf(BLK, BLK), bf(BLK, BLK),
            pltpu.VMEM((8, BLK), jnp.float32),
            dma((steps,)), dma((steps,)), dma((steps,)), dma((steps,)),
            dma((steps, 2)), dma((n,)), dma((n,)), dma((n,)), dma(()), dma(()),
            dma((2 + QUARTERS,)),
            dma((n,)), dma((2 * n,)), dma((n,)), dma((2 * n,)), dma((n, 2)), dma((2 * n,)),
            dma((blocks, QUARTERS)), dma((blocks, QUARTERS)),
            dma((blocks, QUARTERS)), dma((blocks, QUARTERS)),
        ],
        compiler_params=pltpu.CompilerParams(
            collective_id=1, has_side_effects=True, vmem_limit_bytes=60 << 20
        ),
        name="shampoo_step",
    )(codes, table_own, a_part, b_part, table)


def on_device(activations, out_grads, slot_table, exponent_index, damping_index):
    n = lax.axis_size("dp")
    z = lax.axis_index("dp")
    h = lax.axis_index("mp")
    tok = activations.shape[0]
    rows = activations.shape[1] // BLK
    cols = out_grads.shape[1] // BLK
    blocks = rows * cols
    half = BLK // 2
    pieces = BLK // LANE

    act = activations.reshape(tok, rows, 2, half)
    act = jnp.where(h == 0, act[:, :, 0], act[:, :, 1]).reshape(tok, rows * half).T
    grads = out_grads.reshape(tok, cols, pieces, LANE).transpose(2, 0, 1, 3)
    grads = grads.reshape(pieces, tok, cols * LANE)
    table_row = jnp.broadcast_to(
        jnp.pad(slot_table, ((0, 0), (0, LANE - n))), (8, LANE)
    ).astype(jnp.int32)

    spot = lax.rem(z + n - SHIFT * h, n)
    homes = np.asarray([(n * b) // blocks for b in range(blocks)], np.int32)
    lanes = jnp.arange(n, dtype=jnp.int32)
    block_here = jnp.sum(jnp.where(homes == spot, np.arange(blocks, dtype=np.int32), 0))
    slot_here = jnp.sum(jnp.where(lanes == block_here, slot_table[0], 0))
    spots = jnp.stack([lanes == slot_here, lanes == z])
    exps = jnp.sum(jnp.where(spots, exponent_index, 0), axis=1)
    damps = jnp.sum(jnp.where(spots, damping_index, 0), axis=1)
    codes = jnp.stack([exps, damps], axis=1).reshape(4).astype(jnp.int32)

    raw, roots, parts = run_step(codes, slot_table, act, grads, table_row, n, rows, cols)
    total_sq = jnp.sum(parts)
    entries = rows * BLK * cols * BLK * lax.axis_size("mp")
    rescale = lax.rsqrt(total_sq / entries + 1.0)
    update = (raw.astype(jnp.float32) * rescale).astype(jnp.bfloat16)
    return (update, roots[None, None])


def solution(mesh):
    placed = (
        P(("member", "dp"), None),
        P(("member", "dp"), "mp"),
        P(("member", "mp"), None),
        P(("member", "mp"), None),
        P(("member", "mp"), None),
    )
    return jax.shard_map(
        on_device,
        mesh=mesh,
        in_specs=placed,
        out_specs=(P("member", "mp"), P(("member", "mp"), "dp", None, None, None)),
        check_vma=False,
    )
```

time: 942 us -> 561 us (0.60)
  waiting for transfers between devices: 633 us -> 0 us
  Pallas kernels: 0 us -> 516 us
  other arithmetic: 96 us -> 26.1 us
  matrix products: 66.9 us -> 0 us
  blocking collectives: 54 us -> 0 us
  between operations: 40.8 us -> 1.41 us
  starting transfers between devices: 29.4 us -> 0 us
    pallas_call x0 -> x1, Pallas kernels: none -> 516 us  [run_step(): pl.pallas_call(functools.partial(step_kernel, n, rows, cols), out_shape=(...]
    all_to_all x2 -> x0, waiting for transfers between devices: 358 us -> none  [the longest x1 358 us: on_device(): lax.all_to_all(payload, 'dp', split_axis=1, concat_axis=0, tiled=True)]
    all_gather x1 -> x0, waiting for transfers between devices: 275 us -> none  [on_device(): pieces = lax.all_gather(owned_blocks, 'dp', axis=0, tiled=True)]
    dot_general x10 -> x0, matrix products: 66.9 us -> none  [the longest x6 39.1 us: half_dot(): jnp.dot(first.astype(jnp.bfloat16), second.astype(jnp.bfloat16), preferre...]
    dynamic_update_slice x16 -> x0, other arithmetic: 58.8 us -> none  [on_device(): canvas = lax.dynamic_update_slice(canvas, chosen, (row_at, col_at))]
    psum x1 -> x0, blocking collectives: 54 us -> none  [on_device(): total_sq = lax.psum(jnp.sum(owned_wide * owned_wide), ('dp', 'mp'))]
    all_to_all x2 -> x0, starting transfers between devices: 29.2 us -> none  [the longest x1 17.6 us: on_device(): lax.all_to_all(code_rows, 'dp', split_axis=1, concat_axis=0, tiled=True)]
    convert_element_type x3 -> x1, other arithmetic: 16.7 us -> 19.1 us  [on_device(): update = (raw.astype(jnp.float32) * rescale).astype(jnp.bfloat16)]
  transfers between devices with their start and end apart: 3 -> 0, of which waited for: 2 -> 0; matrix products, arithmetic and copies ran while one was open for 3% -> 0% of each run, Pallas kernels for 0% -> 0%
where the time goes in v3:
time: 561 us; the launch traced here: 554 us
  Pallas kernels  516 us (92%)
  other arithmetic  26.1 us (5%)
  local copies, waits for them, and re-layouts  10.4 us (2%)
    pallas_call x1, Pallas kernels, run_step(): pl.pallas_call(functools.partial(step_kernel, n, rows, cols), out_shape=(...  516 us
    convert_element_type x1, other arithmetic, on_device(): update = (raw.astype(jnp.float32) * rescale).astype(jnp.bfloat16)  19.1 us

profile of v3, /device:TPU:69, one launch (start us, length us, event | category | flops | bytes accessed | tf_op | source)
XLA Modules:
  0.0 554.2 jit_solution(740459690580268312)
XLA Ops:
  0.6 1.3 fusion
  1.9 1.9 fusion.1
  3.9 0.7 iota_compare_fusion
  4.5 0.8 select_reduce_fusion.1
  5.4 0.1 copy.23
  5.5 0.7 reshape.35.codes
  6.1 0.7 pad_bitcast_fusion
  6.8 0.6 broadcast_in_dim.48.table_in
  7.4 1.4 reshape.36
  8.8 0.7 fusion.2
  9.5 0.4 copy.30
  10.0 0.4 copy.29
  10.5 0.7 broadcast_select_fusion
  11.2 1.8 copy.26
  13.0 0.1 copy.27
  13.1 1.4 copy.28.b_in
  14.5 516.2 %shampoo_step.1 = (bf16[2048,5120]{1,0:T(8,128)(2,1)}, bf16[2,1024,1024]{2,1,0:T(8,128)(2,1)}, f32[32,8,128]{2,1,0:T(8,128)}) custom-call(s32[4]{0:T(128)} %reshape.35.codes, s32[1,16]{1,0:T(1,128)} %table_own.1, bf16[1024,128]{1,0:T(8,128)(2,1)} %bitcast.19, bf16[8,128,640]{2,1,0:T(8,128)(2,1)} %copy.28.b_in, s32[8,128]{1,0:T(8,128)} %broadcast_in_dim.48.table_in), custom_call_target="tpu_custom_call" | custom-call | tf_op jit(solution)/shard_map/shampoo_step/pallas_call | solution.py:527
  530.8 1.5 reduce_sum.49
  533.0 0.0 copy-start
  533.0 19.1 %multiply_convert_fusion = bf16[2048,5120]{1,0:T(8,128)(2,1)} fusion(bf16[2048,5120]{1,0:T(8,128)(2,1)} %get-tuple-element.5, f32[]{:T(128)S(6)} %rsqrt.3), kind=kLoop, calls=%fused_computation | loop fusion | flops 31457280 | bytes 41943044 | tf_op jit(solution)/shard_map/convert_element_type | solution.py:591
  552.2 0.0 copy-done
  552.2 2.0 copy.32
  (1 shorter events, 0.0 us)
Async XLA Ops:
  533.0 19.2 %copy-start = (bf16[2,1024,1024]{2,1,0:T(8,128)(2,1)S(1)}, bf16[2,1024,1024]{2,1,0:T(8,128)(2,1)}, u32[]{:S(2)}) copy-start(bf16[2,1024,1024]{2,1,0:T(8,128)(2,1)} %get-tuple-element.7) | copy-start | bytes 12582916

commit v4 on v3

--- a/solution.py
+++ b/solution.py
@@ -128,60 +128,82 @@
 
 
 QUARTERS = 4
+VMEM_BASE = 27 << 20
+VMEM_PER_DEVICE = 5 << 10
 
 
 def step_kernel(
     n, rows, cols,
-    codes, table_own, a_in, b_in, table_in,
-    raw, roots, parts,
-    a_all, b_all, table_far, table_smem, acc, shard, payload, home_g, slot_g, upd, part_out,
-    gt, m0, t0, q, r, lane_acc,
-    as_r, ar_r, as_l, ar_l, b_send, b_recv, f_send, f_recv, t_send, t_recv, loc,
-    h_send, h_recv, s_send, s_recv, p_send, p_recv, gs_r, gr_r, gs_l, gr_l,
+    table_own, exps, damps, act, grads,
+    *refs,
 ):
+    raws = refs[:QUARTERS]
+    (
+        roots, parts, a_all, b_in, b_all, table_in, table_far, table_smem, acc, shard,
+        payload, home_g, slot_g, upd, part_out, t0, q, r, lane_acc, as_r, ar_r,
+        as_l, ar_l, b_send, b_recv, f_send, f_recv, t_send, t_recv, loc, h_send, h_recv,
+        s_send, s_recv, p_send, p_recv, gs_r, gr_r, gs_l, gr_l, b_load,
+    ) = refs[QUARTERS:]
     z = lax.axis_index("dp")
     h = lax.axis_index("mp")
     blocks = rows * cols
-    width, tok = a_in.shape
+    tok = act.shape[0]
     half_tok = tok // 2
     half = BLK // 2
+    pieces = BLK // LANE
+    loads = []
+
+    def chunk(at):
+        return a_all.at[pl.ds(pl.multiple_of(at * tok, tok), tok)]
+
+    for row in range(rows):
+        span = pl.ds(pl.multiple_of(row * BLK + h * half, half), half)
+        loads.append(pltpu.make_async_copy(
+            act.at[:, span], chunk(z).at[:, pl.ds(row * half, half)], loc.at[row]
+        ))
+    for col in range(cols):
+        for jj in range(pieces):
+            loads.append(pltpu.make_async_copy(
+                grads.at[:, pl.ds(col * BLK + jj * LANE, LANE)],
+                b_in.at[jj, :, pl.ds(col * LANE, LANE)],
+                b_load.at[jj, col],
+            ))
+    for one in loads:
+        one.start()
+    lane = lax.broadcasted_iota(jnp.int32, (8, LANE), 1)
+    line = jnp.zeros((8, LANE), jnp.int32)
+    for block in range(blocks):
+        line = jnp.where(lane == block, table_own[0, block], line)
+    table_in[...] = line
     right, left = lax.rem(z + 1, n), lax.rem(z + n - 1, n)
     steps = n // 2
     greet_group(n, z, h)
 
-    top, low = pl.ds(0, width // 2), pl.ds(width // 2, width // 2)
     ring = []
+    for one in loads:
+        one.wait()
 
     def ring_send(step):
-        if step == 0:
-            src_r = src_l = a_in
-            at_r = at_l = z
-        else:
-            at_r = lax.rem(z + n - step, n)
-            at_l = lax.rem(z + step, n)
-            src_r, src_l = a_all.at[at_r], a_all.at[at_l]
-        dst_r, dst_l = a_all.at[at_r], a_all.at[at_l]
+        ref_r = chunk(lax.rem(z + n - step, n))
+        ref_l = chunk(lax.rem(z + step, n))
         if step == steps - 1:
-            src_r, dst_r = src_r.at[top], dst_r.at[top]
-            src_l, dst_l = src_l.at[low], dst_l.at[low]
-        one = remote(src_r, dst_r, as_r.at[step], ar_r.at[step], dp=right)
-        two = remote(src_l, dst_l, as_l.at[step], ar_l.at[step], dp=left)
+            ref_r, ref_l = ref_r.at[:, pl.ds(0, half)], ref_l.at[:, pl.ds(half, half)]
+        one = remote(ref_r, ref_r, as_r.at[step], ar_r.at[step], dp=right)
+        two = remote(ref_l, ref_l, as_l.at[step], ar_l.at[step], dp=left)
         one.start()
         two.start()
         ring.extend([one, two])
 
     def ring_recv(step):
-        dst_r = a_all.at[lax.rem(z + n - step - 1, n)]
-        dst_l = a_all.at[lax.rem(z + step + 1, n)]
+        dst_r = chunk(lax.rem(z + n - step - 1, n))
+        dst_l = chunk(lax.rem(z + step + 1, n))
         if step == steps - 1:
-            dst_r, dst_l = dst_r.at[top], dst_l.at[low]
+            dst_r, dst_l = dst_r.at[:, pl.ds(0, half)], dst_l.at[:, pl.ds(half, half)]
         landed(dst_r, ar_r.at[step])
         landed(dst_l, ar_l.at[step])
 
     table = remote(table_in, table_far, t_send, t_recv, mp=1 - h)
     table.start()
-    own_a = pltpu.make_async_copy(a_in, a_all.at[z], loc.at[0])
-    own_a.start()
     ring_send(0)
     parity = lax.rem(z + h, 2)
     h_rows = pl.ds(pl.multiple_of(h * half_tok, half_tok), half_tok)
@@ -223,18 +245,18 @@
     def add_source(at, fresh=False):
         landed(b_all.at[at, 1 - h], f_recv.at[at])
 
-        def body(low_row):
-            span = pl.ds(low_row, STRIPE)
-            got = dot32(a_all[at, span, :], b_all[at].reshape(tok, cols * LANE))
+        right_side = b_all[at].reshape(tok, cols * LANE)
+        for row in range(rows):
+            got = dot32(
+                chunk(at)[:, row * half:(row + 1) * half], right_side, ((0,), (0,))
+            )
+            span = pl.ds(row * half, half)
             if fresh:
                 acc[span, :] = got
             else:
                 acc[span, :] += got
 
-        over_stripes(width, body)
-
     forward(z)
-    own_a.wait()
     for step in range(steps):
         ring_recv(step)
         if step < steps - 1:
@@ -340,8 +362,8 @@
 
     def place_of(block, quarter):
         high = BLK // QUARTERS
-        return raw.at[
-            pl.ds(pl.multiple_of((block // cols) * BLK + quarter * high, high), high),
+        return raws[quarter].at[
+            pl.ds(pl.multiple_of((block // cols) * high, high), high),
             pl.ds(pl.multiple_of(lax.rem(block, cols) * BLK, BLK), BLK),
         ]
 
@@ -358,10 +380,16 @@
             pltpu.make_async_copy(src, dst, loc.at[2 + quarter]),
         )
 
+    home_slot = table_own[0, jnp.minimum(own_block, blocks - 1)]
+
+    for one in ring:
+        one.wait_send()
+    gt, m0 = a_all.at[pl.ds(0, BLK)], a_all.at[pl.ds(BLK, BLK)]
+
     @pl.when(busy)
     def _():
         all_pieces(home_g, h_recv)
-        quartic, order_p, damping = picks_of([codes[0], codes[1]])
+        quartic, order_p, damping = picks_of([exps[0, home_slot], damps[0, home_slot]])
         trace = trace_and_turn(home_g, gt, lane_acc)
         root_into(home_g, roots.at[0], order_p, quartic, damping, trace, None, m0, t0, q, r)
         root_into(home_g, roots.at[1], order_p, quartic, damping, trace, gt, m0, t0, q, r)
@@ -391,7 +419,8 @@
     part_out[...] = tile
     parts[source] = tile
 
-    hop_right, hop_left = n // 2, n - 1 - n // 2
+    def hops(side, quarter):
+        return n // 2 if (quarter < QUARTERS // 2) == (side == 0) else n // 2 - 1
 
     def right_block(i):
         x = lax.rem(spot + n - 1, n)
@@ -404,7 +433,7 @@
 
     def stream(i, quarter, side, phase):
         block, far = (right_block if side == 0 else left_block)(i)
-        limit = hop_right if side == 0 else hop_left
+        limit = hops(side, quarter)
         recv = (gr_r if side == 0 else gr_l).at[block, quarter]
         send = (gs_r if side == 0 else gs_l).at[block, quarter]
         ref = place_of(block, quarter)
@@ -427,7 +456,7 @@
 
     def slot_first():
         all_pieces(slot_g, s_recv)
-        slot_vals["picks"] = picks_of([codes[2], codes[3]])
+        slot_vals["picks"] = picks_of([exps[0, z], damps[0, z]])
         slot_vals["trace"] = trace_and_turn(slot_g, gt, lane_acc)
 
     def slot_unit(side, body):
@@ -478,8 +507,6 @@
             landed(parts.at[chip * 2 + t], p_recv.at[chip * 2 + t])
     landed(parts.at[z * 2 + 1 - h], p_recv.at[z * 2 + 1 - h])
     part_each(lambda go: go.wait_send())
-    for one in ring:
-        one.wait_send()
     for i in range(n // 2):
         same, other = piece(i)
         if i == 0:
@@ -515,80 +542,95 @@
             stream(i, quarter, 1, 2)
 
 
-def run_step(codes, table_own, a_part, b_part, table, n, rows, cols):
-    width, tok = a_part.shape
+def run_step(slot_table, exponent_index, damping_index, activations, out_grads, n, rows, cols, devices):
+    tok = activations.shape[0]
     dma = pltpu.SemaphoreType.DMA
     smem = pl.BlockSpec(memory_space=pltpu.SMEM)
     vmem = pl.BlockSpec(memory_space=pltpu.VMEM)
+    hbm = pl.BlockSpec(memory_space=pltpu.HBM)
     blocks = rows * cols
     half = BLK // 2
+    width = rows * half
+    pieces = BLK // LANE
     bf = lambda *shape: pltpu.VMEM(shape, jnp.bfloat16)
     steps = n // 2
     return pl.pallas_call(
         functools.partial(step_kernel, n, rows, cols),
         out_shape=(
-            jax.ShapeDtypeStruct((rows * BLK, cols * BLK), jnp.bfloat16),
+            *[jax.ShapeDtypeStruct((rows * BLK // QUARTERS, cols * BLK), jnp.bfloat16)] * QUARTERS,
             jax.ShapeDtypeStruct((2, BLK, BLK), jnp.bfloat16),
             jax.ShapeDtypeStruct((2 * n, 8, LANE), jnp.float32),
         ),
-        in_specs=[smem, smem, vmem, vmem, vmem],
-        out_specs=(pl.BlockSpec(memory_space=pl.ANY), vmem, vmem),
+        in_specs=[smem, smem, smem, hbm, hbm],
+        out_specs=(*[pl.BlockSpec(memory_space=pl.ANY)] * QUARTERS, vmem, vmem),
         scratch_shapes=[
-            bf(n, width, tok), bf(n, 2, tok // 2, cols * LANE),
-            pltpu.VMEM((8, LANE), jnp.int32), pltpu.SMEM((8, LANE), jnp.int32),
+            bf(n * tok, width), bf(pieces, tok, cols * LANE), bf(n, 2, tok // 2, cols * LANE),
+            pltpu.VMEM((8, LANE), jnp.int32), pltpu.VMEM((8, LANE), jnp.int32), pltpu.SMEM((8, LANE), jnp.int32),
             pltpu.VMEM((width, cols * LANE), jnp.float32),
             bf(blocks, half, LANE), bf(n, half, LANE), bf(BLK, BLK), bf(BLK, BLK), bf(BLK, BLK),
             pltpu.VMEM((8, LANE), jnp.float32),
-            bf(BLK, BLK), bf(BLK, BLK), bf(BLK, BLK), bf(BLK, BLK), bf(BLK, BLK),
+            bf(BLK, BLK), bf(BLK, BLK), bf(BLK, BLK),
             pltpu.VMEM((8, BLK), jnp.float32),
             dma((steps,)), dma((steps,)), dma((steps,)), dma((steps,)),
             dma((steps, 2)), dma((n,)), dma((n,)), dma((n,)), dma(()), dma(()),
             dma((2 + QUARTERS,)),
             dma((n,)), dma((2 * n,)), dma((n,)), dma((2 * n,)), dma((n, 2)), dma((2 * n,)),
             dma((blocks, QUARTERS)), dma((blocks, QUARTERS)),
-            dma((blocks, QUARTERS)), dma((blocks, QUARTERS)),
+            dma((blocks, QUARTERS)), dma((blocks, QUARTERS)), dma((pieces, cols)),
         ],
         compiler_params=pltpu.CompilerParams(
-            collective_id=1, has_side_effects=True, vmem_limit_bytes=60 << 20
+            collective_id=1, has_side_effects=True, vmem_limit_bytes=VMEM_BASE + VMEM_PER_DEVICE * devices
         ),
         name="shampoo_step",
-    )(codes, table_own, a_part, b_part, table)
-
-
-def on_device(activations, out_grads, slot_table, exponent_index, damping_index):
+    )(slot_table, exponent_index, damping_index, activations, out_grads)
+
+
+def rescale_kernel(entries, parts, *refs):
+    out = refs[-1]
+    total_sq = jnp.sum(jnp.sum(parts[...], axis=0), keepdims=True)
+    scale = lax.rsqrt(total_sq / entries + 1.0)
+    g = lax.rem(pl.program_id(0), 2 * QUARTERS)
+    for quarter in range(QUARTERS):
+        @pl.when(g // 2 == quarter)
+        def _(quarter=quarter):
+            out[...] = (refs[quarter][...].astype(jnp.float32) * scale).astype(jnp.bfloat16)
+
+
+def rescaled(raws, parts, entries):
+    height, width = raws[0].shape
+    high = BLK // QUARTERS // 2
+    picks = [
+        pl.BlockSpec(
+            (high, width),
+            lambda g, quarter=quarter: (
+                2 * (g // (2 * QUARTERS)) + jnp.clip(g % (2 * QUARTERS) - 2 * quarter, 0, 1), 0
+            ),
+        )
+        for quarter in range(QUARTERS)
+    ]
+    return pl.pallas_call(
+        functools.partial(rescale_kernel, entries),
+        out_shape=jax.ShapeDtypeStruct((height * QUARTERS, width), jnp.bfloat16),
+        grid=(height * QUARTERS // high,),
+        in_specs=[pl.BlockSpec(parts.shape, lambda g: (0, 0, 0))] + picks,
+        out_specs=pl.BlockSpec((high, width), lambda g: (g, 0)),
+        compiler_params=pltpu.CompilerParams(vmem_limit_bytes=16 << 20),
+        cost_estimate=pl.CostEstimate(
+            flops=8 * height * width, bytes_accessed=16 * height * width, transcendentals=0
+        ),
+        name="rescaled",
+    )(parts, *raws)
+
+
+def on_device(devices, activations, out_grads, slot_table, exponent_index, damping_index):
     n = lax.axis_size("dp")
-    z = lax.axis_index("dp")
-    h = lax.axis_index("mp")
-    tok = activations.shape[0]
     rows = activations.shape[1] // BLK
     cols = out_grads.shape[1] // BLK
-    blocks = rows * cols
-    half = BLK // 2
-    pieces = BLK // LANE
-
-    act = activations.reshape(tok, rows, 2, half)
-    act = jnp.where(h == 0, act[:, :, 0], act[:, :, 1]).reshape(tok, rows * half).T
-    grads = out_grads.reshape(tok, cols, pieces, LANE).transpose(2, 0, 1, 3)
-    grads = grads.reshape(pieces, tok, cols * LANE)
-    table_row = jnp.broadcast_to(
-        jnp.pad(slot_table, ((0, 0), (0, LANE - n))), (8, LANE)
-    ).astype(jnp.int32)
-
-    spot = lax.rem(z + n - SHIFT * h, n)
-    homes = np.asarray([(n * b) // blocks for b in range(blocks)], np.int32)
-    lanes = jnp.arange(n, dtype=jnp.int32)
-    block_here = jnp.sum(jnp.where(homes == spot, np.arange(blocks, dtype=np.int32), 0))
-    slot_here = jnp.sum(jnp.where(lanes == block_here, slot_table[0], 0))
-    spots = jnp.stack([lanes == slot_here, lanes == z])
-    exps = jnp.sum(jnp.where(spots, exponent_index, 0), axis=1)
-    damps = jnp.sum(jnp.where(spots, damping_index, 0), axis=1)
-    codes = jnp.stack([exps, damps], axis=1).reshape(4).astype(jnp.int32)
-
-    raw, roots, parts = run_step(codes, slot_table, act, grads, table_row, n, rows, cols)
-    total_sq = jnp.sum(parts)
+    *raws, roots, parts = run_step(
+        slot_table, exponent_index, damping_index, activations, out_grads, n, rows, cols, devices
+    )
     entries = rows * BLK * cols * BLK * lax.axis_size("mp")
-    rescale = lax.rsqrt(total_sq / entries + 1.0)
-    update = (raw.astype(jnp.float32) * rescale).astype(jnp.bfloat16)
+    update = rescaled(raws, parts, float(entries))
     return (update, roots[None, None])
 
 
@@ -601,7 +643,7 @@
         P(("member", "mp"), None),
     )
     return jax.shard_map(
-        on_device,
+        functools.partial(on_device, mesh.size),
         mesh=mesh,
         in_specs=placed,
         out_specs=(P("member", "mp"), P(("member", "mp"), "dp", None, None, None)),

time: 561 us -> 523 us (0.932); the launches traced: 554 us -> 523 us
  other arithmetic: 26.1 us -> 0 us
    convert_element_type x1 -> x0, other arithmetic: 19.1 us -> none  [on_device(): update = (raw.astype(jnp.float32) * rescale).astype(jnp.bfloat16)]
    pallas_call x1, Pallas kernels: 516 us -> 504 us  [run_step(): pl.pallas_call(functools.partial(step_kernel, n, rows, cols), out_shape=(...]
    pallas_call x0 -> x1, Pallas kernels: none -> 11.9 us  [rescaled(): pl.pallas_call(functools.partial(rescale_kernel, entries), out_shape=jax....]
where the time goes in v4:
time: 523 us
  Pallas kernels  516 us (99%)
  local copies, waits for them, and re-layouts  6.33 us (1%)
    pallas_call x1, Pallas kernels, run_step(): pl.pallas_call(functools.partial(step_kernel, n, rows, cols), out_shape=(...  504 us
    pallas_call x1, Pallas kernels, rescaled(): pl.pallas_call(functools.partial(rescale_kernel, entries), out_shape=jax....  11.9 us

profile of v4, /device:TPU:69, one launch (start us, length us, event | category | flops | bytes accessed | tf_op | source)
XLA Modules:
  0.0 523.2 jit_solution(7596192010065763256)
XLA Ops:
  0.6 0.0 copy-start
  0.6 1.3 copy-done
  1.9 0.0 copy-start.1
  2.0 1.0 copy-done.1
  3.0 0.0 copy-start.2
  3.0 0.7 copy-done.2
  3.6 0.0 copy-start.3
  3.6 0.7 copy-done.3
  4.3 0.0 copy-start.4
  4.3 0.7 copy-done.4
  5.0 504.3 %shampoo_step.1 = (bf16[512,5120]{1,0:T(8,128)(2,1)S(1)}, bf16[512,5120]{1,0:T(8,128)(2,1)S(1)}, bf16[512,5120]{1,0:T(8,128)(2,1)S(1)}, bf16[512,5120]{1,0:T(8,1...) custom-call(s32[1,16]{1,0:T(1,128)S(1)} %copy-done.2, s32[1,16]{1,0:T(1,128)S(1)} %copy-done.3, ...), custom_call_target="tpu_custom_call" | custom-call | tf_op jit(solution)/shard_map/shampoo_step/pallas_call | solution.py:557
  509.3 11.9 %rescaled.1 = bf16[2048,5120]{1,0:T(8,128)(2,1)} custom-call(f32[32,8,128]{2,1,0:T(8,128)S(1)} %get-tuple-element.8.parts, bf16[512,5120]{1,0:T(8,128)(2,1)S(1)} %get-tuple-element.9.refs_0_, bf16[512,5120]{1,0:T(8,128)(2,1)S(1)} %get-tuple-element.10.refs_1_, bf16[512,5120]{1,0:T(8,128)(2,1)S(1)} %get-tuple-element.11.refs_2_, ...), custom_call_target="tpu_custom_call" | custom-call | flops 20971520 | bytes 41943040 | tf_op jit(solution)/shard_map/rescaled/pallas_call | solution.py:611
  521.2 2.0 copy.8
Async XLA Ops:
  0.6 1.3 copy-start
  1.9 1.0 copy-start.1
  3.0 0.7 copy-start.2
  3.6 0.7 copy-start.3
  4.3 0.7 copy-start.4

commit v5 on v4

--- a/solution.py
+++ b/solution.py
@@ -128,13 +128,15 @@
 
 
 QUARTERS = 4
+SLOT_MASK = 255
 VMEM_BASE = 27 << 20
 VMEM_PER_DEVICE = 5 << 10
+RESCALE_LIMIT = 28 << 20
 
 
 def step_kernel(
     n, rows, cols,
-    table_own, exps, damps, act, grads,
+    packed, act, grads,
     *refs,
 ):
     raws = refs[:QUARTERS]
@@ -170,10 +172,14 @@
             ))
     for one in loads:
         one.start()
+    def codes_at(slot):
+        word = packed[0, slot]
+        return (word >> 8) & 15, (word >> 12) & 15
+
     lane = lax.broadcasted_iota(jnp.int32, (8, LANE), 1)
     line = jnp.zeros((8, LANE), jnp.int32)
     for block in range(blocks):
-        line = jnp.where(lane == block, table_own[0, block], line)
+        line = jnp.where(lane == block, packed[0, block] & SLOT_MASK, line)
     table_in[...] = line
     right, left = lax.rem(z + 1, n), lax.rem(z + n - 1, n)
     steps = n // 2
@@ -183,28 +189,29 @@
     for one in loads:
         one.wait()
 
-    def ring_send(step):
-        ref_r = chunk(lax.rem(z + n - step, n))
-        ref_l = chunk(lax.rem(z + step, n))
-        if step == steps - 1:
-            ref_r, ref_l = ref_r.at[:, pl.ds(0, half)], ref_l.at[:, pl.ds(half, half)]
-        one = remote(ref_r, ref_r, as_r.at[step], ar_r.at[step], dp=right)
-        two = remote(ref_l, ref_l, as_l.at[step], ar_l.at[step], dp=left)
+    def ring_part(at, row):
+        return chunk(at).at[:, pl.ds(row * half, half)]
+
+    def ring_rows(step, side):
+        return (side,) if step == steps - 1 else tuple(range(rows))
+
+    def ring_send(step, side, row):
+        at = lax.rem(z + n - step, n) if side == 0 else lax.rem(z + step, n)
+        ref = ring_part(at, row)
+        send, recv, to = (as_r, ar_r, right) if side == 0 else (as_l, ar_l, left)
+        one = remote(ref, ref, send.at[step, row], recv.at[step, row], dp=to)
         one.start()
-        two.start()
-        ring.extend([one, two])
-
-    def ring_recv(step):
-        dst_r = chunk(lax.rem(z + n - step - 1, n))
-        dst_l = chunk(lax.rem(z + step + 1, n))
-        if step == steps - 1:
-            dst_r, dst_l = dst_r.at[:, pl.ds(0, half)], dst_l.at[:, pl.ds(half, half)]
-        landed(dst_r, ar_r.at[step])
-        landed(dst_l, ar_l.at[step])
+        ring.append(one)
+
+    def ring_recv(step, side, row):
+        at = lax.rem(z + n - step - 1, n) if side == 0 else lax.rem(z + step + 1, n)
+        landed(ring_part(at, row), (ar_r if side == 0 else ar_l).at[step, row])
 
     table = remote(table_in, table_far, t_send, t_recv, mp=1 - h)
     table.start()
-    ring_send(0)
+    for row in range(rows):
+        for side in range(2):
+            ring_send(0, side, row)
     parity = lax.rem(z + h, 2)
     h_rows = pl.ds(pl.multiple_of(h * half_tok, half_tok), half_tok)
     o_rows = pl.ds(pl.multiple_of((1 - h) * half_tok, half_tok), half_tok)
@@ -258,9 +265,15 @@
 
     forward(z)
     for step in range(steps):
-        ring_recv(step)
-        if step < steps - 1:
-            ring_send(step + 1)
+        if step == steps - 1:
+            add_source(lax.rem(z + step, n))
+            add_source(lax.rem(z + n - step, n))
+        for row in range(rows):
+            for side in range(2):
+                if row in ring_rows(step, side):
+                    ring_recv(step, side, row)
+                if step < steps - 1 and row in ring_rows(step + 1, side):
+                    ring_send(step + 1, side, row)
         if step == steps - 1:
             forward(lax.rem(z + steps, n))
         else:
@@ -268,7 +281,7 @@
             forward(lax.rem(z + n - step - 1, n))
         if step == 0:
             add_source(z, True)
-        else:
+        elif step < steps - 1:
             add_source(lax.rem(z + step, n))
             add_source(lax.rem(z + n - step, n))
     add_source(lax.rem(z + steps, n))
@@ -329,7 +342,7 @@
         pick = jnp.int32(0)
         filled = jnp.int32(0)
         for block in range(blocks):
-            served = jnp.where(m == h, table_own[0, block], table_smem[0, block])
+            served = jnp.where(m == h, packed[0, block] & SLOT_MASK, table_smem[0, block])
             pick = jnp.where(served == slot, block, pick)
             filled = jnp.where(served == slot, 1, filled)
         part = shard[pick]
@@ -380,7 +393,7 @@
             pltpu.make_async_copy(src, dst, loc.at[2 + quarter]),
         )
 
-    home_slot = table_own[0, jnp.minimum(own_block, blocks - 1)]
+    home_slot = packed[0, jnp.minimum(own_block, blocks - 1)] & SLOT_MASK
 
     for one in ring:
         one.wait_send()
@@ -389,7 +402,7 @@
     @pl.when(busy)
     def _():
         all_pieces(home_g, h_recv)
-        quartic, order_p, damping = picks_of([exps[0, home_slot], damps[0, home_slot]])
+        quartic, order_p, damping = picks_of(codes_at(home_slot))
         trace = trace_and_turn(home_g, gt, lane_acc)
         root_into(home_g, roots.at[0], order_p, quartic, damping, trace, None, m0, t0, q, r)
         root_into(home_g, roots.at[1], order_p, quartic, damping, trace, gt, m0, t0, q, r)
@@ -456,7 +469,7 @@
 
     def slot_first():
         all_pieces(slot_g, s_recv)
-        slot_vals["picks"] = picks_of([exps[0, z], damps[0, z]])
+        slot_vals["picks"] = picks_of(codes_at(z))
         slot_vals["trace"] = trace_and_turn(slot_g, gt, lane_acc)
 
     def slot_unit(side, body):
@@ -542,7 +555,7 @@
             stream(i, quarter, 1, 2)
 
 
-def run_step(slot_table, exponent_index, damping_index, activations, out_grads, n, rows, cols, devices):
+def run_step(packed, activations, out_grads, n, rows, cols, devices):
     tok = activations.shape[0]
     dma = pltpu.SemaphoreType.DMA
     smem = pl.BlockSpec(memory_space=pltpu.SMEM)
@@ -561,7 +574,7 @@
             jax.ShapeDtypeStruct((2, BLK, BLK), jnp.bfloat16),
             jax.ShapeDtypeStruct((2 * n, 8, LANE), jnp.float32),
         ),
-        in_specs=[smem, smem, smem, hbm, hbm],
+        in_specs=[smem, hbm, hbm],
         out_specs=(*[pl.BlockSpec(memory_space=pl.ANY)] * QUARTERS, vmem, vmem),
         scratch_shapes=[
             bf(n * tok, width), bf(pieces, tok, cols * LANE), bf(n, 2, tok // 2, cols * LANE),
@@ -571,7 +584,7 @@
             pltpu.VMEM((8, LANE), jnp.float32),
             bf(BLK, BLK), bf(BLK, BLK), bf(BLK, BLK),
             pltpu.VMEM((8, BLK), jnp.float32),
-            dma((steps,)), dma((steps,)), dma((steps,)), dma((steps,)),
+            dma((steps, rows)), dma((steps, rows)), dma((steps, rows)), dma((steps, rows)),
             dma((steps, 2)), dma((n,)), dma((n,)), dma((n,)), dma(()), dma(()),
             dma((2 + QUARTERS,)),
             dma((n,)), dma((2 * n,)), dma((n,)), dma((2 * n,)), dma((n, 2)), dma((2 * n,)),
@@ -582,39 +595,51 @@
             collective_id=1, has_side_effects=True, vmem_limit_bytes=VMEM_BASE + VMEM_PER_DEVICE * devices
         ),
         name="shampoo_step",
-    )(slot_table, exponent_index, damping_index, activations, out_grads)
-
-
-def rescale_kernel(entries, parts, *refs):
-    out = refs[-1]
+    )(packed, activations, out_grads)
+
+
+def rescale_kernel(entries, high, parts, *refs):
+    raws, (out, buffers, sems) = refs[:QUARTERS], refs[QUARTERS:]
     total_sq = jnp.sum(jnp.sum(parts[...], axis=0), keepdims=True)
     scale = lax.rsqrt(total_sq / entries + 1.0)
-    g = lax.rem(pl.program_id(0), 2 * QUARTERS)
+    groups = raws[0].shape[0] // high
+    per_row = BLK // QUARTERS // high
+
+    def out_copy(quarter, group):
+        at = (group // per_row) * BLK + quarter * (BLK // QUARTERS) + lax.rem(group, per_row) * high
+        return pltpu.make_async_copy(
+            buffers.at[group], out.at[pl.ds(pl.multiple_of(at, high), high)], sems.at[group]
+        )
+
     for quarter in range(QUARTERS):
-        @pl.when(g // 2 == quarter)
-        def _(quarter=quarter):
-            out[...] = (refs[quarter][...].astype(jnp.float32) * scale).astype(jnp.bfloat16)
+        def step(group, carry, quarter=quarter):
+            if quarter > 0:
+                out_copy(quarter - 1, group).wait()
+            span = pl.ds(pl.multiple_of(group * high, high), high)
+            wide = raws[quarter][span, :].astype(jnp.float32)
+            buffers[group] = (wide * scale).astype(jnp.bfloat16)
+            out_copy(quarter, group).start()
+            return carry
+
+        lax.fori_loop(0, groups, step, 0)
+    for group in range(groups):
+        out_copy(QUARTERS - 1, group).wait()
 
 
 def rescaled(raws, parts, entries):
     height, width = raws[0].shape
     high = BLK // QUARTERS // 2
-    picks = [
-        pl.BlockSpec(
-            (high, width),
-            lambda g, quarter=quarter: (
-                2 * (g // (2 * QUARTERS)) + jnp.clip(g % (2 * QUARTERS) - 2 * quarter, 0, 1), 0
-            ),
-        )
-        for quarter in range(QUARTERS)
-    ]
+    vmem = pl.BlockSpec(memory_space=pltpu.VMEM)
     return pl.pallas_call(
-        functools.partial(rescale_kernel, entries),
+        functools.partial(rescale_kernel, entries, high),
         out_shape=jax.ShapeDtypeStruct((height * QUARTERS, width), jnp.bfloat16),
-        grid=(height * QUARTERS // high,),
-        in_specs=[pl.BlockSpec(parts.shape, lambda g: (0, 0, 0))] + picks,
-        out_specs=pl.BlockSpec((high, width), lambda g: (g, 0)),
-        compiler_params=pltpu.CompilerParams(vmem_limit_bytes=16 << 20),
+        in_specs=[vmem] * (1 + QUARTERS),
+        out_specs=pl.BlockSpec(memory_space=pl.ANY),
+        scratch_shapes=[
+            pltpu.VMEM((height // high, high, width), jnp.bfloat16),
+            pltpu.SemaphoreType.DMA((height // high,)),
+        ],
+        compiler_params=pltpu.CompilerParams(vmem_limit_bytes=RESCALE_LIMIT),
         cost_estimate=pl.CostEstimate(
             flops=8 * height * width, bytes_accessed=16 * height * width, transcendentals=0
         ),
@@ -627,7 +652,7 @@
     rows = activations.shape[1] // BLK
     cols = out_grads.shape[1] // BLK
     *raws, roots, parts = run_step(
-        slot_table, exponent_index, damping_index, activations, out_grads, n, rows, cols, devices
+        slot_table + exponent_index * 256 + damping_index * 4096, activations, out_grads, n, rows, cols, devices
     )
     entries = rows * BLK * cols * BLK * lax.axis_size("mp")
     update = rescaled(raws, parts, float(entries))

time: 523 us -> 509 us (0.973)
  Pallas kernels: 516 us -> 503 us
    pallas_call x1, Pallas kernels: 504 us -> 495 us  [run_step(): pl.pallas_call(functools.partial(step_kernel, n, rows, cols), out_shape=(...]
where the time goes in v5:
time: 509 us; the launch traced here: 508 us
  Pallas kernels  503 us (99%)
    pallas_call x1, Pallas kernels, run_step(): pl.pallas_call(functools.partial(step_kernel, n, rows, cols), out_shape=(...  495 us

profile of v5, /device:TPU:69, one launch (start us, length us, event | category | flops | bytes accessed | tf_op | source)
XLA Modules:
  0.0 508.4 jit_solution(586876684897652609)
XLA Ops:
  0.6 0.7 multiply_add_fusion.packed
  1.3 0.0 copy-start
  1.3 1.3 copy-done
  2.6 0.0 copy-start.1
  2.6 1.0 copy-done.1
  3.7 495.2 %shampoo_step.1 = (bf16[512,5120]{1,0:T(8,128)(2,1)S(1)}, bf16[512,5120]{1,0:T(8,128)(2,1)S(1)}, bf16[512,5120]{1,0:T(8,128)(2,1)S(1)}, bf16[512,5120]{1,0:T(8,1...) custom-call(s32[1,16]{1,0:T(1,128)S(1)} %multiply_add_fusion.packed, ...), custom_call_target="tpu_custom_call" | custom-call | tf_op jit(solution)/shard_map/shampoo_step/pallas_call | solution.py:570
  498.9 7.5 %rescaled.1 = bf16[2048,5120]{1,0:T(8,128)(2,1)} custom-call(f32[32,8,128]{2,1,0:T(8,128)S(1)} %get-tuple-element.8.parts, bf16[512,5120]{1,0:T(8,128)(2,1)S(1)} %get-tuple-element.9.refs_0_, bf16[512,5120]{1,0:T(8,128)(2,1)S(1)} %get-tuple-element.10.refs_1_, bf16[512,5120]{1,0:T(8,128)(2,1)S(1)} %get-tuple-element.11.refs_2_, ...), custom_call_target="tpu_custom_call" | custom-call | flops 20971520 | bytes 41943040 | tf_op jit(solution)/shard_map/rescaled/pallas_call | solution.py:633
  506.4 2.0 copy.8
Async XLA Ops:
  1.3 1.3 copy-start
  2.6 1.0 copy-start.1

commit v6 on v5

--- a/solution.py
+++ b/solution.py
@@ -99,15 +99,14 @@
     return quartic, order, damping
 
 
-def greet_group(n, z, h):
+def greet_neighbours(n, z, h):
     barrier = pltpu.get_barrier_semaphore()
     pl.semaphore_signal(barrier, inc=1, device_id={"mp": 1 - h}, device_id_type=MESH)
-    for o in range(1, n):
-        for t in range(2):
-            pl.semaphore_signal(
-                barrier, inc=1, device_id={"dp": lax.rem(z + o, n), "mp": t}, device_id_type=MESH
-            )
-    pl.semaphore_wait(barrier, 2 * n - 1)
+    for o in (1, n - 1):
+        pl.semaphore_signal(
+            barrier, inc=1, device_id={"dp": lax.rem(z + o, n)}, device_id_type=MESH
+        )
+    pl.semaphore_wait(barrier, 3)
 
 
 def remote(src, dst, send, recv, **to):
@@ -131,7 +130,7 @@
 SLOT_MASK = 255
 VMEM_BASE = 27 << 20
 VMEM_PER_DEVICE = 5 << 10
-RESCALE_LIMIT = 28 << 20
+RESCALE_BASE = 22 << 20
 
 
 def step_kernel(
@@ -144,7 +143,7 @@
         roots, parts, a_all, b_in, b_all, table_in, table_far, table_smem, acc, shard,
         payload, home_g, slot_g, upd, part_out, t0, q, r, lane_acc, as_r, ar_r,
         as_l, ar_l, b_send, b_recv, f_send, f_recv, t_send, t_recv, loc, h_send, h_recv,
-        s_send, s_recv, p_send, p_recv, gs_r, gr_r, gs_l, gr_l, b_load,
+        s_send, s_recv, p_send, p_recv, gs_r, gr_r, gs_l, gr_l, b_load, tok_r, tok_l,
     ) = refs[QUARTERS:]
     z = lax.axis_index("dp")
     h = lax.axis_index("mp")
@@ -183,7 +182,19 @@
     table_in[...] = line
     right, left = lax.rem(z + 1, n), lax.rem(z + n - 1, n)
     steps = n // 2
-    greet_group(n, z, h)
+    greet_neighbours(n, z, h)
+
+    def tell(t):
+        pl.semaphore_signal(tok_r.at[t], inc=1, device_id={"dp": right}, device_id_type=MESH)
+        if t < steps - 1:
+            pl.semaphore_signal(tok_l.at[t], inc=1, device_id={"dp": left}, device_id_type=MESH)
+
+    def hear(t):
+        pl.semaphore_wait(tok_r.at[t], 1)
+        if t < steps - 1:
+            pl.semaphore_wait(tok_l.at[t], 1)
+
+    tell(0)
 
     ring = []
     for one in loads:
@@ -216,34 +227,42 @@
     h_rows = pl.ds(pl.multiple_of(h * half_tok, half_tok), half_tok)
     o_rows = pl.ds(pl.multiple_of((1 - h) * half_tok, half_tok), half_tok)
 
-    def piece(i):
-        chip = lax.rem(z + parity + 2 * i, n)
+    def piece(o):
+        chip = lax.rem(z + o, n)
         block = b_in.at[chip // 2]
-        same = remote(block.at[h_rows], b_all.at[z, h], b_send.at[i, 0], b_recv.at[z], dp=chip, mp=h)
+        same = remote(block.at[h_rows], b_all.at[z, h], b_send.at[o, 0], b_recv.at[z], dp=chip, mp=h)
         other = remote(
-            block.at[o_rows], b_all.at[z, 1 - h], b_send.at[i, 1], b_recv.at[z], dp=chip, mp=1 - h
+            block.at[o_rows], b_all.at[z, 1 - h], b_send.at[o, 1], b_recv.at[z], dp=chip, mp=1 - h
         )
         return same, other
 
-    self_chip = parity == 0
-    order = []
-    for i in range(n // 4):
-        order.extend([i, n // 2 - 1 - i])
-    for i in order:
-        same, other = piece(i)
-        if i == 0:
-            @pl.when(self_chip)
-            def _():
-                pltpu.make_async_copy(
-                    b_in.at[z // 2].at[h_rows], b_all.at[z, h], b_recv.at[z]
-                ).start()
-
-            @pl.when(jnp.logical_not(self_chip))
-            def _():
+    def piece_go(o, start):
+        @pl.when(parity == o % 2)
+        def _():
+            same, other = piece(o)
+            if o == 0:
+                if start:
+                    pltpu.make_async_copy(
+                        b_in.at[z // 2].at[h_rows], b_all.at[z, h], b_recv.at[z]
+                    ).start()
+            elif start:
                 same.start()
+            else:
+                same.wait_send()
+            if start:
+                other.start()
+            else:
+                other.wait_send()
+
+    piece_go(0, True)
+    for t in range(steps):
+        hear(t)
+        if t < steps - 1:
+            tell(t + 1)
+            piece_go(t + 1, True)
+            piece_go(n - t - 1, True)
         else:
-            same.start()
-        other.start()
+            piece_go(steps, True)
 
     def forward(at):
         landed(b_all.at[at, h], b_recv.at[at])
@@ -520,16 +539,8 @@
             landed(parts.at[chip * 2 + t], p_recv.at[chip * 2 + t])
     landed(parts.at[z * 2 + 1 - h], p_recv.at[z * 2 + 1 - h])
     part_each(lambda go: go.wait_send())
-    for i in range(n // 2):
-        same, other = piece(i)
-        if i == 0:
-            @pl.when(jnp.logical_not(self_chip))
-            def _():
-                same.wait_send()
-        else:
-            same.wait_send()
-        other.wait_send()
     for o in range(n):
+        piece_go(o, False)
         at = lax.rem(z + o, n)
         remote(b_all.at[at, h], b_all.at[at, h], f_send.at[at], f_recv.at[at], mp=1 - h).wait_send()
         home_go(o, False)
@@ -585,11 +596,12 @@
             bf(BLK, BLK), bf(BLK, BLK), bf(BLK, BLK),
             pltpu.VMEM((8, BLK), jnp.float32),
             dma((steps, rows)), dma((steps, rows)), dma((steps, rows)), dma((steps, rows)),
-            dma((steps, 2)), dma((n,)), dma((n,)), dma((n,)), dma(()), dma(()),
+            dma((n, 2)), dma((n,)), dma((n,)), dma((n,)), dma(()), dma(()),
             dma((2 + QUARTERS,)),
             dma((n,)), dma((2 * n,)), dma((n,)), dma((2 * n,)), dma((n, 2)), dma((2 * n,)),
             dma((blocks, QUARTERS)), dma((blocks, QUARTERS)),
             dma((blocks, QUARTERS)), dma((blocks, QUARTERS)), dma((pieces, cols)),
+            pltpu.SemaphoreType.REGULAR((steps,)), pltpu.SemaphoreType.REGULAR((steps,)),
         ],
         compiler_params=pltpu.CompilerParams(
             collective_id=1, has_side_effects=True, vmem_limit_bytes=VMEM_BASE + VMEM_PER_DEVICE * devices
@@ -598,8 +610,10 @@
     )(packed, activations, out_grads)
 
 
-def rescale_kernel(entries, high, parts, *refs):
-    raws, (out, buffers, sems) = refs[:QUARTERS], refs[QUARTERS:]
+def rescale_kernel(entries, high, parts, roots, *refs):
+    raws, (out, roots_out, buffers, sems, root_sem) = refs[:QUARTERS], refs[QUARTERS:]
+    root_copy = pltpu.make_async_copy(roots, roots_out, root_sem)
+    root_copy.start()
     total_sq = jnp.sum(jnp.sum(parts[...], axis=0), keepdims=True)
     scale = lax.rsqrt(total_sq / entries + 1.0)
     groups = raws[0].shape[0] // high
@@ -624,27 +638,32 @@
         lax.fori_loop(0, groups, step, 0)
     for group in range(groups):
         out_copy(QUARTERS - 1, group).wait()
-
-
-def rescaled(raws, parts, entries):
+    root_copy.wait()
+
+
+def rescaled(raws, parts, roots, entries, devices):
     height, width = raws[0].shape
     high = BLK // QUARTERS // 2
     vmem = pl.BlockSpec(memory_space=pltpu.VMEM)
     return pl.pallas_call(
         functools.partial(rescale_kernel, entries, high),
-        out_shape=jax.ShapeDtypeStruct((height * QUARTERS, width), jnp.bfloat16),
-        in_specs=[vmem] * (1 + QUARTERS),
-        out_specs=pl.BlockSpec(memory_space=pl.ANY),
+        out_shape=(
+            jax.ShapeDtypeStruct((height * QUARTERS, width), jnp.bfloat16),
+            jax.ShapeDtypeStruct(roots.shape, jnp.bfloat16),
+        ),
+        in_specs=[vmem] * (2 + QUARTERS),
+        out_specs=(pl.BlockSpec(memory_space=pltpu.HBM), pl.BlockSpec(memory_space=pltpu.HBM)),
         scratch_shapes=[
             pltpu.VMEM((height // high, high, width), jnp.bfloat16),
             pltpu.SemaphoreType.DMA((height // high,)),
+            pltpu.SemaphoreType.DMA(()),
         ],
-        compiler_params=pltpu.CompilerParams(vmem_limit_bytes=RESCALE_LIMIT),
+        compiler_params=pltpu.CompilerParams(vmem_limit_bytes=RESCALE_BASE + VMEM_PER_DEVICE * devices),
         cost_estimate=pl.CostEstimate(
             flops=8 * height * width, bytes_accessed=16 * height * width, transcendentals=0
         ),
         name="rescaled",
-    )(parts, *raws)
+    )(parts, roots, *raws)
 
 
 def on_device(devices, activations, out_grads, slot_table, exponent_index, damping_index):
@@ -655,7 +674,7 @@
         slot_table + exponent_index * 256 + damping_index * 4096, activations, out_grads, n, rows, cols, devices
     )
     entries = rows * BLK * cols * BLK * lax.axis_size("mp")
-    update = rescaled(raws, parts, float(entries))
+    update, roots = rescaled(raws, parts, roots, float(entries), devices)
     return (update, roots[None, None])
 
 

time: 509 us -> 504 us (level)
  no operation moved by 1% of the time
where the time goes in v6:
time: 504 us
  Pallas kernels  500 us (99%)
    pallas_call x1, Pallas kernels, run_step(): pl.pallas_call(functools.partial(step_kernel, n, rows, cols), out_shape=(...  492 us

profile of v6, /device:TPU:69, one launch (start us, length us, event | category | flops | bytes accessed | tf_op | source)
XLA Modules:
  0.0 503.8 jit_solution(17988229001450137001)
XLA Ops:
  0.6 0.7 multiply_add_fusion.packed
  1.3 0.0 copy-start
  1.3 1.3 copy-done
  2.6 0.0 copy-start.1
  2.6 1.0 copy-done.1
  3.7 491.5 %shampoo_step.1 = (bf16[512,5120]{1,0:T(8,128)(2,1)S(1)}, bf16[512,5120]{1,0:T(8,128)(2,1)S(1)}, bf16[512,5120]{1,0:T(8,128)(2,1)S(1)}, bf16[512,5120]{1,0:T(8,1...) custom-call(s32[1,16]{1,0:T(1,128)S(1)} %multiply_add_fusion.packed, ...), custom_call_target="tpu_custom_call" | custom-call | tf_op jit(solution)/shard_map/shampoo_step/pallas_call | solution.py:581
  495.2 8.4 %rescaled.1 = (bf16[2048,5120]{1,0:T(8,128)(2,1)}, bf16[2,1024,1024]{2,1,0:T(8,128)(2,1)}) custom-call(f32[32,8,128]{2,1,0:T(8,128)S(1)} %get-tuple-element.10.parts, bf16[2,1024,1024]{2,1,0:T(8,128)(2,1)S(1)} %get-tuple-element.11.roots, bf16[512,5120]{1,0:T(8,128)(2,1)S(1)} %get-tuple-element.12.refs_0_, bf16[512,5120]{1,0:T(8,128)(2,1)S(1)} %get-tuple-element.13.refs_1_, ...), custom_call_target="tpu_custom_call" | custom-call | flops 20971520 | bytes 41943040 | tf_op jit(solution)/shard_map/rescaled/pallas_call | solution.py:648
Async XLA Ops:
  1.3 1.3 copy-start
  2.6 1.0 copy-start.1

commit v7 on v6

--- a/solution.py
+++ b/solution.py
@@ -126,10 +126,10 @@
     return order + [0]
 
 
-QUARTERS = 4
+QUARTERS = 8
 SLOT_MASK = 255
 VMEM_BASE = 27 << 20
-VMEM_PER_DEVICE = 5 << 10
+VMEM_PER_DEVICE = 7 << 10
 RESCALE_BASE = 22 << 20
 
 

time: 504 us -> 504 us (level)
  no operation moved by 1% of the time
where the time goes in v7:
time: 504 us
  Pallas kernels  500 us (99%)
    pallas_call x1, Pallas kernels, run_step(): pl.pallas_call(functools.partial(step_kernel, n, rows, cols), out_shape=(...  491 us

profile of v7, /device:TPU:69, one launch (start us, length us, event | category | flops | bytes accessed | tf_op | source)
XLA Modules:
  0.0 504.2 jit_solution(3487485630353263633)
XLA Ops:
  0.6 0.7 multiply_add_fusion.packed
  1.3 0.0 copy-start
  1.3 1.3 copy-done
  2.6 0.0 copy-start.1
  2.6 1.0 copy-done.1
  3.7 490.8 %shampoo_step.1 = (bf16[256,5120]{1,0:T(8,128)(2,1)S(1)}, bf16[256,5120]{1,0:T(8,128)(2,1)S(1)}, bf16[256,5120]{1,0:T(8,128)(2,1)S(1)}, bf16[256,5120]{1,0:T(8,1...) custom-call(s32[1,16]{1,0:T(1,128)S(1)} %multiply_add_fusion.packed,, ...), custom_call_target="tpu_custom_call" | custom-call | tf_op jit(solution)/shard_map/shampoo_step/pallas_call | solution.py:581
  494.5 9.4 %rescaled.1 = (bf16[2048,5120]{1,0:T(8,128)(2,1)}, bf16[2,1024,1024]{2,1,0:T(8,128)(2,1)}) custom-call(f32[32,8,128]{2,1,0:T(8,128)S(1)} %get-tuple-element.14.parts, bf16[2,1024,1024]{2,1,0:T(8,128)(2,1)S(1)} %get-tuple-element.15.roots, bf16[256,5120]{1,0:T(8,128)(2,1)S(1)} %get-tuple-element.16.refs_0_, bf16[256,5120]{1,0:T(8,128)(2,1)S(1)} %get-tuple-element.17.refs_1_, ...), custom_call_target="tpu_custom_call" | custom-call | flops 10485760 | bytes 20971520 | tf_op jit(solution)/shard_map/rescaled/pallas_call | solution.py:648
Async XLA Ops:
  1.3 1.3 copy-start
  2.6 1.0 copy-start.1
